TPU v7x, 256 devices: a whole 4x4x8 slice. The times are simulated.
256 devices in a mesh: rep: 2 (over core), dp: 128 (over x, y, z).
Axes of the slice: x: 4, y: 4, z: 8, core: 2. Of those that a mesh axis runs over, the one named last changes fastest.
Arguments:
- x: bfloat16 [256, 2048, 512], P(('rep', 'dp')), parts along dimension 0
- dy: bfloat16 [256, 2048, 512], P(('rep', 'dp')), parts along dimension 0
- w_gate: bfloat16 [2, 512, 1536], replicated
- w_up: bfloat16 [2, 512, 1536], replicated
- w_down: bfloat16 [2, 1536, 512], replicated
- m_w_gate: float32 [2, 512, 1536], replicated
- m_w_up: float32 [2, 512, 1536], replicated
- m_w_down: float32 [2, 1536, 512], replicated
- v_w_gate: float32 [2, 512, 1536], replicated
- v_w_up: float32 [2, 512, 1536], replicated
- v_w_down: float32 [2, 1536, 512], replicated
Outputs:
- output 1: bfloat16 [4, 512, 1536], P('rep'), parts along dimension 0
- output 2: bfloat16 [4, 512, 1536], P('rep'), parts along dimension 0
- output 3: bfloat16 [4, 1536, 512], P('rep'), parts along dimension 0
- output 4: float32 [4, 512, 1536], P('rep'), parts along dimension 0
- output 5: float32 [4, 512, 1536], P('rep'), parts along dimension 0
- output 6: float32 [4, 1536, 512], P('rep'), parts along dimension 0
- output 7: float32 [4, 512, 1536], P('rep'), parts along dimension 0
- output 8: float32 [4, 512, 1536], P('rep'), parts along dimension 0
- output 9: float32 [4, 1536, 512], P('rep'), parts along dimension 0
There are 2 independent parts. A program takes and returns all parts, laid end to end along the dimension named above; an argument that names none is the same for every part.
All inputs are finite; a program needn't handle non-finite values.
Results may differ from a plain program's by a relative error of at most 0.022.
Values are sent between devices in bfloat16 or wider.
A program may use at most 768 MiB of HBM per device.

v0:
```python
import functools

import jax
import jax.numpy as jnp
from jax import lax
from jax.experimental import pallas as pl
from jax.experimental.pallas import tpu as pltpu
from jax.sharding import PartitionSpec as P

MESH = pl.DeviceIdType.MESH
DIMS = (4, 4, 8)
BLOCK = 512
TILE = 1024
FORWARD_TILE = 512
PERIOD = (("inputs",), ("back 0",), ("back 1",), ("down", "gate", "up"))
TICKS = len(PERIOD)
TN = (((0,), (0,)), ((), ()))
NT = (((1,), (1,)), ((), ()))
BF16, F32 = jnp.bfloat16, jnp.float32


def adamw(w, m, v, g):
    m = 0.9 * m + 0.1 * g
    v = 0.95 * v + 0.05 * g * g
    step = m * lax.rsqrt(v + 1e-8) + 0.1 * w
    return (w - 0.02 * step).astype(jnp.bfloat16), m, v


def ds(start, size, multiple=None):
    if isinstance(start, int):
        return pl.ds(start, size)
    return pl.ds(pl.multiple_of(start, multiple or size), size)


class Torus:
    def __init__(self):
        i = lax.axis_index("dp")
        nx, ny, nz = DIMS
        self.at = (lax.div(i, ny * nz), lax.rem(lax.div(i, nz), ny), lax.rem(i, nz))

    def shifted(self, axis, by):
        n = DIMS[axis]
        return lax.rem(self.at[axis] + (by % n), n)

    def device(self, axis, by):
        to = list(self.at)
        to[axis] = self.shifted(axis, by)
        return {"dp": (to[0] * DIMS[1] + to[1]) * DIMS[2] + to[2]}

    def barrier(self):
        sem = pltpu.get_barrier_semaphore()
        peers = [(axis, by) for axis in range(3) for by in range(1, DIMS[axis])]
        for axis, by in peers:
            pl.semaphore_signal(sem, inc=1, device_id=self.device(axis, by), device_id_type=MESH)
        return lambda: pl.semaphore_wait(sem, len(peers))


class Step:
    def __init__(self, start, finish):
        self.start, self.finish = start, finish


def rows_loop(rows, lanes, body):
    size = min(rows, max(16, 16 * (512 // lanes)))
    if rows == size:
        body(0, size)
        return

    def one(i, _):
        body(pl.multiple_of(i * size, size), size)
        return 0

    lax.fori_loop(0, rows // size, one, 0)


class Exchange:
    def __init__(self, torus, order, chained, chunk, rx, p32, pb, r32, rb, sems, sites):
        self.torus, self.order, self.chained = torus, order, chained
        self.chunk = chunk
        self.rx1, self.rx2, self.rx3 = rx
        self.p32, self.pb, self.r32, self.rb = p32, pb, r32, rb
        self.send_sems, self.recv_sems = sems
        self.sites = sites
        n1, n2, n3 = (DIMS[a] for a in order)
        self.rows1 = BLOCK // n1
        self.lanes2 = BLOCK // n2
        self.rows3 = self.rows1 // n3
        self.steps = self._steps()

    def _site(self):
        s = self.sites[0]
        self.sites[0] += 1
        return s

    def _copy(self, c, site, src, dst, axis, by):
        slot = c
        pltpu.make_async_remote_copy(
            src_ref=src,
            dst_ref=dst,
            send_sem=self.send_sems.at[slot, site],
            recv_sem=self.recv_sems.at[slot, site],
            device_id=self.torus.device(axis, by),
            device_id_type=MESH,
        ).start()

    def _wait(self, c, site, like, recv):
        sem = (self.recv_sems if recv else self.send_sems).at[c, site]
        pltpu.make_async_copy(like, like, sem).wait()

    def _chain(self, axis, rows, lanes, send_ref, own, rx, total):
        n = DIMS[axis]
        k = n // 2
        half = rows // 2
        ways = ((1, 0, 0), (-1, 1, half))
        steps = []
        for s in range(1, k + 1):
            sites = [self._site() for _ in ways]

            def start(c, s=s, sites=sites):
                for (way, w, h0), site in zip(ways, sites, strict=True):
                    t = self.torus.shifted(axis, way * (k + 1 - s))
                    dst = rx(c, w, s - 1)
                    if s == 1:
                        self._copy(c, site, send_ref(c, t, h0, half), dst.at[ds(h0, half), :], axis, way)
                    elif s == 2:
                        o0 = half - h0
                        self._copy(c, site, rx(c, w, 0).at[ds(h0, half), :], dst.at[ds(h0, half), :], axis, way)
                        self._copy(c, site, send_ref(c, t, o0, half), dst.at[ds(o0, half), :], axis, way)
                    else:
                        self._copy(c, site, rx(c, w, s - 2), dst, axis, way)

            def finish(c, s=s, sites=sites):
                for (way, w, h0), site in zip(ways, sites, strict=True):
                    got = rx(c, w, s - 1)
                    part = got.at[ds(h0, half), :] if s == 1 else got
                    self._wait(c, site, part, True)
                    if s < k:
                        t = self.torus.shifted(axis, way * (k - s))
                        first, count = (h0, half) if s == 1 else (0, rows)

                        def add(r0, size, got=got, t=t, first=first):
                            at = ds(first + r0, size, 16)
                            got[at, :] = (got[at, :].astype(F32) + own(c, t, first + r0, size)).astype(BF16)

                        rows_loop(count, lanes, add)
                if s == k:
                    me = self.torus.shifted(axis, 0)
                    for first in (0, half):

                        def add(r0, size, first=first):
                            at = ds(first + r0, size, 16)
                            value = own(c, me, first + r0, size)
                            for way, w, h0 in ways:
                                if k > 1 or h0 == first:
                                    value = value + rx(c, w, k - 1)[at, :].astype(F32)
                            total(c, first + r0, size, value)

                        rows_loop(half, lanes, add)
                for (way, w, h0), site in zip(ways, sites, strict=True):
                    got = rx(c, w, s - 1)
                    self._wait(c, site, got.at[ds(h0, half), :] if s == 1 else got, False)

            steps.append(Step(start, finish))
        return steps

    def _chain_gather(self, axis, rows, block):
        n = DIMS[axis]
        k = n // 2
        half = rows // 2
        ways = ((1, 0), (-1, half))
        steps = []
        for s in range(1, k + 1):
            sites = [self._site() for _ in ways]

            def start(c, s=s, sites=sites):
                for (way, h0), site in zip(ways, sites, strict=True):
                    t = self.torus.shifted(axis, -way * (s - 1))
                    ref = block(c, t, h0, half) if s == k else block(c, t, 0, rows)
                    self._copy(c, site, ref, ref, axis, way)

            def finish(c, s=s, sites=sites):
                for recv in (True, False):
                    for (way, h0), site in zip(ways, sites, strict=True):
                        t = self.torus.shifted(axis, -way * s)
                        self._wait(c, site, block(c, t, h0, half) if s == k else block(c, t, 0, rows), recv)

            steps.append(Step(start, finish))
        return steps

    def _direct(self, axis, rows, lanes, send_ref, own, rx, total):
        n = DIMS[axis]
        site = self._site()

        def start(c):
            for by in range(1, n):
                t = self.torus.shifted(axis, by)
                self._copy(c, site, send_ref(c, t), rx(c).at[by - 1], axis, by)

        def finish(c):
            self._wait(c, site, rx(c), True)

            def add(r0, size):
                value = own(c, r0, size)
                for i in range(n - 1):
                    value = value + rx(c)[i, ds(r0, size, 16), :].astype(F32)
                total(c, r0, size, value)

            rows_loop(rows, lanes, add)
            self._wait(c, site, rx(c), False)

        return [Step(start, finish)]

    def _direct_gather(self, axis, mine, like):
        n = DIMS[axis]
        site = self._site()

        def start(c):
            for by in range(1, n):
                self._copy(c, site, mine(c), mine(c), axis, by)

        def finish(c):
            self._wait(c, site, like(c), True)
            self._wait(c, site, like(c), False)

        return [Step(start, finish)]

    def _steps(self):
        a1, a2, a3 = self.order
        rows1, lanes2, rows3 = self.rows1, self.lanes2, self.rows3
        at = [self.torus.at[a] for a in self.order]
        chunk = self.chunk

        def block1(c, t, r0, n):
            return chunk(c).at[ds(t * rows1 + r0, n, 16), :]

        def own1(c, t, r0, n):
            return chunk(c)[ds(t * rows1 + r0, n, 16), :].astype(F32)

        def total1(c, r0, n, value):
            at_ = ds(r0, n, 16)
            self.p32[c % 2, at_, :] = value
            self.pb[c % 2, at_, :] = value.astype(BF16)

        steps = self._chain(a1, rows1, BLOCK, block1, own1, lambda c, w, s: self.rx1.at[c, w, s], total1)

        def own2(c, t, r0, n):
            return self.p32[c % 2, ds(r0, n, 16), ds(t * lanes2, lanes2)]

        def total2(c, r0, n, value):
            at_ = ds(r0, n, 16)
            self.r32[c % 2, at_, :] = value
            self.rb[c % 2, at_, :] = value.astype(BF16)

        if self.chained:
            steps += self._chain(
                a2,
                rows1,
                lanes2,
                lambda c, t, r0, n: self.pb.at[c % 2, ds(r0, n, 16), ds(t * lanes2, lanes2)],
                own2,
                lambda c, w, s: self.rx2.at[c, w, s],
                total2,
            )
        else:
            steps += self._direct(
                a2,
                rows1,
                lanes2,
                lambda c, t: self.pb.at[c % 2, :, ds(t * lanes2, lanes2)],
                lambda c, r0, n: own2(c, at[1], r0, n),
                lambda c: self.rx2.at[c],
                total2,
            )

        def final(c):
            return chunk(c).at[ds(at[0] * rows1 + at[2] * rows3, rows3, 16), ds(at[1] * lanes2, lanes2)]

        def total3(c, r0, n, value):
            final(c)[ds(r0, n, 16), :] = value.astype(BF16)

        steps += self._direct(
            a3,
            rows3,
            lanes2,
            lambda c, t: self.rb.at[c % 2, ds(t * rows3, rows3, 16), :],
            lambda c, r0, n: self.r32[c % 2, ds(at[2] * rows3 + r0, n, 16), :],
            lambda c: self.rx3.at[c],
            total3,
        )
        steps += self._direct_gather(a3, final, lambda c: self.rx3.at[c])

        def block2(c, t, r0, n):
            return chunk(c).at[ds(at[0] * rows1 + r0, n, 16), ds(t * lanes2, lanes2)]

        if self.chained:
            steps += self._chain_gather(a2, rows1, block2)
        else:
            steps += self._direct_gather(a2, lambda c: block2(c, at[1], 0, rows1), lambda c: self.rx2.at[c])
        steps += self._chain_gather(a1, rows1, block1)
        return steps

    @staticmethod
    def scratch(order, chained, chunks):
        n1, n2, n3 = (DIMS[a] for a in order)
        rows1, lanes2 = BLOCK // n1, BLOCK // n2
        rx2 = (chunks, 2, n2 // 2, rows1, lanes2) if chained else (chunks, n2 - 1, rows1, lanes2)
        return [
            pltpu.VMEM((chunks, 2, n1 // 2, rows1, BLOCK), BF16),
            pltpu.VMEM(rx2, BF16),
            pltpu.VMEM((chunks, n3 - 1, rows1 // n3, lanes2), BF16),
            pltpu.VMEM((2, rows1, BLOCK), F32),
            pltpu.VMEM((2, rows1, BLOCK), BF16),
            pltpu.VMEM((2, rows1, lanes2), F32),
            pltpu.VMEM((2, rows1, lanes2), BF16),
        ]

    @staticmethod
    def n_sites(order, chained):
        k1, k2 = DIMS[order[0]] // 2, DIMS[order[1]] // 2
        return 4 * k1 + (4 * k2 if chained else 2) + 2


COLOURS = (((0, 1, 2), True), ((1, 0, 2), True), ((2, 0, 1), False))


def dot(a, b, dims=(((1,), (0,)), ((), ()))):
    return lax.dot_general(a, b, dims, preferred_element_type=F32)


def inverse_rms(wide):
    return lax.rsqrt(jnp.mean(wide * wide, -1, keepdims=True) + 1e-6)


def normed(h):
    wide = h.astype(F32)
    return (wide * inverse_rms(wide)).astype(BF16)


def sigmoid(x):
    return 0.5 * jnp.tanh(0.5 * x) + 0.5


def tiles(rows, size, body):
    def one(i, _):
        body(pl.ds(pl.multiple_of(i * size, size), size))
        return 0

    lax.fori_loop(0, rows // size, one, 0)


class Compute:
    def __init__(self, weights, states, dh, a, by, da):
        self.w_gate, self.w_up, self.w_down = weights
        self.states = states
        self.dh = dh
        self.a = a
        self.by = by
        self.da = da

    def forward(self, number):
        rows, ff = self.a.shape[0], self.w_gate.shape[2]

        def body(at):
            h = self.states[number, at, :]
            a = normed(h)
            out = None
            for f in range(0, ff, BLOCK):
                columns = pl.ds(f, BLOCK)
                gate = dot(a, self.w_gate[number, :, columns])
                up = dot(a, self.w_up[number, :, columns])
                part = dot((gate * sigmoid(gate) * up).astype(BF16), self.w_down[number, columns, :])
                out = part if out is None else out + part
            h = h + out.astype(BF16)
            self.states[number + 1, at, :] = h
            self.a[at, :] = normed(h)

        tiles(rows, min(FORWARD_TILE, rows), body)

    def back(self, number, block, tile):
        columns = ds(block * BLOCK, BLOCK)
        size = min(TILE, self.a.shape[0] // 2)
        at = pl.ds(tile * size, size)
        a = self.a[at, :]
        gate = dot(a, self.w_gate[number, :, columns])
        up = dot(a, self.w_up[number, :, columns])
        by = dot(self.dh[at, :], self.w_down[number, columns, :], NT).astype(BF16).astype(F32)
        s = sigmoid(gate)
        silu = gate * s
        self.by[0, at, :] = (silu * up).astype(BF16)
        self.by[1, at, :] = (by * up * (s + silu * (1.0 - s))).astype(BF16)
        self.by[2, at, :] = (by * silu).astype(BF16)

    def gradient(self, which, into):
        if which == 0:
            into[...] = dot(self.by[0], self.dh[...], TN).astype(BF16)
        else:
            into[...] = dot(self.a[...], self.by[which], TN).astype(BF16)

    def inputs(self, number, block):
        columns = ds(block * BLOCK, BLOCK)
        rows = self.a.shape[0]

        def body(at):
            part = dot(self.by[1, at, :], self.w_gate[number, :, columns], NT)
            part = part + dot(self.by[2, at, :], self.w_up[number, :, columns], NT)
            self.da[at, :] = jnp.where(block == 0, 0.0, self.da[at, :]) + part

        tiles(rows, min(TILE, rows), body)

    def below(self, number):
        rows = self.a.shape[0]

        def body(at):
            wide = self.states[number, at, :].astype(F32)
            by = self.da[at, :].astype(BF16).astype(F32)
            scale = inverse_rms(wide)
            by = by * scale - wide * (scale * scale * scale * jnp.mean(by * wide, -1, keepdims=True))
            self.dh[at, :] = self.dh[at, :] + by.astype(BF16)
            self.a[at, :] = normed(self.states[number - 1, at, :])

        tiles(rows, min(256, rows), body)


def train_kernel(x, dy, w_gate, w_up, w_down, o_gate, o_up, o_down, *scratch):
    (s_gate, s_up, s_down, states, dh, a, by, da, g), scratch = scratch[:9], scratch[9:]
    scratch, (send_sems, recv_sems, out_sems, in_sems) = scratch[:-4], scratch[-4:]
    layers, _, ff = w_gate.shape
    blocks = ff // BLOCK
    chunks = layers * blocks
    assert layers == 2
    torus = Torus()
    loads = [pltpu.make_async_copy(x.at[0], states.at[0], in_sems.at[0])]
    for number in range(layers):
        for i, (src, dst) in enumerate(((w_gate, s_gate), (w_up, s_up), (w_down, s_down))):
            loads.append(pltpu.make_async_copy(src.at[number], dst.at[number], in_sems.at[1 + 3 * number + i]))
    loads.append(pltpu.make_async_copy(dy.at[0], dh, in_sems.at[1 + 3 * layers]))
    for copy in loads:
        copy.start()
    barrier = torus.barrier()
    compute = Compute((s_gate, s_up, s_down), states, dh, a, by, da)
    for copy in loads[:4]:
        copy.wait()
    compute.forward(0)
    for copy in loads[4:]:
        copy.wait()
    barrier()

    sites, exchanges = [0], []
    for k, (order, chained) in enumerate(COLOURS):
        rx, temporary = scratch[7 * k : 7 * k + 3], scratch[7 * k + 3 : 7 * k + 7]
        exchanges.append(Exchange(torus, order, chained, lambda c, k=k: g.at[c, k], rx, *temporary, (send_sems, recv_sems), sites))
    longest = max(len(e.steps) for e in exchanges)

    def save(c, k):
        number, j = layers - 1 - lax.div(c, blocks), lax.rem(c, blocks)
        place = o_down.at[number, ds(j * BLOCK, BLOCK), :] if k == 0 else (o_gate, o_up)[k - 1].at[number, :, ds(j * BLOCK, BLOCK)]
        return pltpu.make_async_copy(g.at[c, k], place, out_sems.at[c, k])

    def tick(s, period):
        for stage in range(s, longest + 1, TICKS):
            c = period - 1 - stage // TICKS

            @pl.when((c >= 0) & (c < chunks))
            def _(c=c, stage=stage):
                for k, e in enumerate(exchanges):
                    if 1 <= stage <= len(e.steps):
                        e.steps[stage - 1].finish(c)
                        if stage == len(e.steps):
                            save(c, k).start()
                for e in exchanges:
                    if stage < len(e.steps):
                        e.steps[stage].start(c)

    def work(name, period):
        number, block = layers - 1 - lax.div(period, blocks), lax.rem(period, blocks)
        if name == "inputs":
            before = period - 1

            @pl.when((before >= 0) & (before < chunks - blocks))
            def _():
                compute.inputs(layers - 1 - lax.div(before, blocks), lax.rem(before, blocks))

            @pl.when((period > 0) & (period < chunks) & (block == 0))
            def _():
                compute.below(number + 1)

            return

        @pl.when(period < chunks)
        def _():
            if name.startswith("back"):
                compute.back(number, block, int(name[5:]))
            else:
                which = ("down", "gate", "up").index(name)
                compute.gradient(which, g.at[period, which])

    def body(period, _):
        for s in range(TICKS):
            tick(s, period)
            for name in PERIOD[s]:
                work(name, period)
        return 0

    lax.fori_loop(0, chunks + 1 + longest // TICKS, body, 0)
    for c in range(chunks):
        for k in range(3):
            save(c, k).wait()


def gradients(x, dy, gate, up, down):
    layers, d, ff = gate.shape
    tokens = x.shape[1]
    chunks = layers * ff // BLOCK
    scratch = [
        *(pltpu.VMEM(w.shape, BF16) for w in (gate, up, down)),
        pltpu.VMEM((layers, tokens, d), BF16),
        pltpu.VMEM((tokens, d), BF16),
        pltpu.VMEM((tokens, d), BF16),
        pltpu.VMEM((3, tokens, BLOCK), BF16),
        pltpu.VMEM((tokens, d), F32),
        pltpu.VMEM((chunks, 3, BLOCK, BLOCK), BF16),
    ]
    n_sites = 0
    for order, chained in COLOURS:
        scratch += Exchange.scratch(order, chained, chunks)
        n_sites += Exchange.n_sites(order, chained)
    scratch += [pltpu.SemaphoreType.DMA((chunks, n_sites))] * 2
    scratch += [pltpu.SemaphoreType.DMA((chunks, 3)), pltpu.SemaphoreType.DMA((2 + 3 * layers,))]
    return pl.pallas_call(
        train_kernel,
        out_shape=[jax.ShapeDtypeStruct(w.shape, BF16) for w in (gate, up, down)],
        in_specs=[pl.BlockSpec(memory_space=pl.ANY)] * 5,
        out_specs=[pl.BlockSpec(memory_space=pl.ANY)] * 3,
        scratch_shapes=scratch,
        compiler_params=pltpu.CompilerParams(collective_id=0, has_side_effects=True, vmem_limit_bytes=63 << 20),
        name="gradients",
    )(x, dy, gate, up, down)


def solution(mesh):
    def step(x, dy, *arrays):
        weights, m, v = (arrays[i : i + 3] for i in (0, 3, 6))
        summed = [g.astype(F32) for g in gradients(x, dy, *weights)]
        new = [adamw(w.astype(F32), m, v, g) for w, m, v, g in zip(weights, m, v, summed, strict=True)]
        return tuple(one[which] for which in range(3) for one in new)

    return jax.shard_map(
        step,
        mesh=mesh,
        in_specs=(P(("rep", "dp"), None, None),) * 2 + (P(None, None, None),) * 9,
        out_specs=(P("rep", None, None),) * 9,
        check_vma=False,
    )
```

profile of v0, /device:TPU:2, one launch (start us, length us, event | category | flops | bytes accessed | tf_op | source)
XLA Modules:
  0.0 216.1 jit_solution(13843041660054106926)
XLA Ops:
  0.6 181.0 %gradients.1 = (bf16[2,512,1536]{2,1,0:T(8,128)(2,1)}, bf16[2,512,1536]{2,1,0:T(8,128)(2,1)}, bf16[2,1536,512]{2,1,0:T(8,128)(2,1)}) custom-call(bf16[1,2048,512]{2,1,0:T(8,128)(2,1)} %x.1, bf16[1,2048,512]{2,1,0:T(8,128)(2,1)} %dy.1, bf16[2,512,1536]{2,1,0:T(8,128)(2,1)} %w_gate.1, bf16[2,512,1536]{2,1,0:T(8,128)(2,1)} %w_up.1, bf16[2,1536,512]{2,1,0:T(8,128)(2,1)} %w_down.1), custom_call_target="tpu_custom_call" | custom-call | tf_op jit(solution)/shard_map/gradients/pallas_call | solution.py:529
  181.6 0.0 copy-start
  181.7 0.0 copy-start.1
  181.7 25.3 %fusion.2 = (bf16[2,512,1536]{2,1,0:T(8,128)(2,1)}, f32[2,512,1536]{2,1,0:T(8,128)}, f32[2,512,1536]{2,1,0:T(8,128)}, bf16[2,512,1536]{2,1,0:T(8,128)(2,1)}, f32...) fusion(bf16[2,512,1536]{2,1,0:T(8,128)(2,1)} %w_gate.1, bf16[2,512,1536]{2,1,0:T(8,128)(2,1)} %get-tuple-element.12, ...), kind=kLoop, calls=%fused_computation.14 | loop fusion | flops 50331648 | bytes 69206016 | tf_op jit(solution)/shard_map/convert_element_type | solution.py:26
  207.0 0.0 copy-done
  207.0 0.0 copy-done.1
  207.0 9.1 %fusion.10 = (bf16[2,1536,512]{2,1,0:T(8,128)(2,1)}, f32[2,1536,512]{2,1,0:T(8,128)}, f32[2,1536,512]{2,1,0:T(8,128)}) fusion(bf16[2,1536,512]{2,1,0:T(8,128)(2,1)S(1)} %copy-done, bf16[2,1536,512]{2,1,0:T(8,128)(2,1)} %get-tuple-element.14, f32[2,1536,512]{2,1,0:T(8,128)S(1)} %copy-done.1, f32[2,1536,512]{2,1,0:T(8,128)} %param.18), kind=kLoop, calls=%fused_computation.22 | loop fusion | flops 25165824 | bytes 34603008 | tf_op jit(solution)/shard_map/convert_element_type | solution.py:26
Async XLA Ops:
  181.6 25.4 %copy-start = (bf16[2,1536,512]{2,1,0:T(8,128)(2,1)S(1)}, bf16[2,1536,512]{2,1,0:T(8,128)(2,1)}, u32[]{:S(2)}) copy-start(bf16[2,1536,512]{2,1,0:T(8,128)(2,1)} %w_down.1) | copy-start | bytes 9437188
  181.7 25.4 %copy-start.1 = (f32[2,1536,512]{2,1,0:T(8,128)S(1)}, f32[2,1536,512]{2,1,0:T(8,128)}, u32[]{:S(2)}) copy-start(f32[2,1536,512]{2,1,0:T(8,128)} %param.21) | copy-start | bytes 18874372
where the time goes:
time: 216 us
  Pallas kernels  181 us (84%)
  other arithmetic  34.4 us (16%)
    pallas_call x1, Pallas kernels, gradients(): pl.pallas_call(train_kernel, out_shape=[jax.ShapeDtypeStruct(w.shape, BF1...  181 us
    convert_element_type x2, other arithmetic, adamw(): return ((w - 0.02 * step).astype(jnp.bfloat16), m, v)  34.4 us

commit v1 on v0

v1 whole, which is shorter than its diff:
```python
import functools

import jax
import jax.numpy as jnp
from jax import lax
from jax.experimental import pallas as pl
from jax.experimental.pallas import tpu as pltpu
from jax.sharding import PartitionSpec as P

MESH = pl.DeviceIdType.MESH
DIMS = (4, 4, 8)
BLOCK = 512
TILE = 512
PIECE = 128
STRIP = 32
SLOTS = 3
OUTPUTS = 4
PERIOD = (
    "below",
    (2, 8, 3), (0, 7, 3),
    "back 0",
    (2, 5, 2), (1, 1, 1), (0, 9, 4), (1, 7, 3), (2, 2, 1),
    "back 1",
    (0, 2, 1), (1, 9, 4), (2, 11, 4), (0, 5, 2),
    "back 2",
    (0, 8, 3), (2, 6, 2), (1, 5, 2), (1, 2, 1), (2, 9, 3),
    "back 3",
    (2, 3, 1), (0, 3, 1), (1, 8, 3),
    "up",
    (2, 7, 2), (0, 10, 4), (1, 10, 4), (2, 12, 4), (2, 0, 0),
    "down",
    (0, 0, 0), (2, 10, 3), (0, 6, 2), (0, 4, 1), (1, 3, 1), (2, 4, 1),
    "gate",
    (1, 0, 0), (2, 1, 0),
    "inputs 0",
    (1, 6, 2),
    "inputs 1",
    (0, 1, 0), (1, 4, 1),
)
VMEM_LIMIT = UPDATE_LIMIT = 29_200_000
TN = (((0,), (0,)), ((), ()))
NT = (((1,), (1,)), ((), ()))
BF16, F32 = jnp.bfloat16, jnp.float32


def ds(start, size, multiple=None):
    if isinstance(start, int):
        return pl.ds(start, size)
    return pl.ds(pl.multiple_of(start, multiple or size), size)


class Torus:
    def __init__(self):
        i = lax.axis_index("dp")
        nx, ny, nz = DIMS
        self.at = (lax.div(i, ny * nz), lax.rem(lax.div(i, nz), ny), lax.rem(i, nz))
        self._places, self._devices = {}, {}
        for axis, n in enumerate(DIMS):
            for by in range(n):
                self._places[axis, by] = place = lax.rem(self.at[axis] + by, n) if by else self.at[axis]
                to = list(self.at)
                to[axis] = place
                self._devices[axis, by] = (to[0] * ny + to[1]) * nz + to[2]

    def shifted(self, axis, by):
        return self._places[axis, by % DIMS[axis]]

    def device(self, axis, by):
        return {"dp": self._devices[axis, by % DIMS[axis]]}

    def barrier(self):
        sem = pltpu.get_barrier_semaphore()
        peers = [(axis, by) for axis in range(3) for by in range(1, DIMS[axis])]
        for axis, by in peers:
            pl.semaphore_signal(sem, inc=1, device_id=self.device(axis, by), device_id_type=MESH)
        return lambda: pl.semaphore_wait(sem, len(peers))


class Step:
    def __init__(self, start, finish):
        self.start, self.finish = start, finish


def rows_loop(rows, lanes, body):
    size = min(rows, 32 * 1024 // lanes)
    for r0 in range(0, rows, size):
        body(r0, size)


class Exchange:
    def __init__(self, torus, order, chained, chunk, rx, p32, pb, r32, rb, sems, sites):
        self.torus, self.order, self.chained = torus, order, chained
        self.chunk = chunk
        self.rx1, self.rx2, self.rx3 = rx
        self.p32, self.pb, self.r32, self.rb = p32, pb, r32, rb
        self.send_sems, self.recv_sems = sems
        self.sites = sites
        n1, n2, n3 = (DIMS[a] for a in order)
        self.rows1 = BLOCK // n1
        self.lanes2 = BLOCK // n2
        self.rows3 = self.rows1 // n3
        self.steps = self._steps()

    def _site(self):
        s = self.sites[0]
        self.sites[0] += 1
        return s

    def _copy(self, c, site, src, dst, axis, by):
        pltpu.make_async_remote_copy(
            src_ref=src,
            dst_ref=dst,
            send_sem=self.send_sems.at[lax.rem(c, SLOTS), site],
            recv_sem=self.recv_sems.at[lax.rem(c, SLOTS), site],
            device_id=self.torus.device(axis, by),
            device_id_type=MESH,
        ).start()

    def _arrived(self, c, site, like):
        pltpu.make_async_copy(like, like, self.recv_sems.at[lax.rem(c, SLOTS), site]).wait()

    def _left(self, c, site, like):
        pltpu.make_async_copy(like, like, self.send_sems.at[lax.rem(c, SLOTS), site]).wait()

    def _chain(self, axis, rows, lanes, send_ref, own, rx, total):
        n = DIMS[axis]
        k = n // 2
        half = rows // 2
        ways = ((1, 0, 0), (-1, 1, half))
        steps = []
        for s in range(1, k + 1):
            site = self._site()

            def start(c, s=s, site=site):
                for way, w, h0 in ways:
                    t = self.torus.shifted(axis, way * (k + 1 - s))
                    dst = rx(c, s - 1).at[w]
                    if s == 1:
                        self._copy(c, site, send_ref(c, t, h0, half), dst.at[ds(h0, half), :], axis, way)
                    elif s == 2:
                        o0 = half - h0
                        self._copy(c, site, rx(c, 0).at[w, ds(h0, half), :], dst.at[ds(h0, half), :], axis, way)
                        self._copy(c, site, send_ref(c, t, o0, half), dst.at[ds(o0, half), :], axis, way)
                    else:
                        self._copy(c, site, rx(c, s - 2).at[w], dst, axis, way)

            def finish(c, s=s, site=site):
                got = rx(c, s - 1)
                like = got.at[0] if s == 1 else got
                self._arrived(c, site, like)
                if s < k:
                    for way, w, h0 in ways:
                        t = self.torus.shifted(axis, way * (k - s))
                        first, count = (h0, half) if s == 1 else (0, rows)

                        def add(r0, size, w=w, t=t, first=first):
                            at = pl.ds(first + r0, size)
                            got[w, at, :] = (got[w, at, :].astype(F32) + own(c, t, first + r0, size)).astype(BF16)

                        rows_loop(count, lanes, add)
                else:
                    me = self.torus.shifted(axis, 0)
                    for first in (0, half):

                        def add(r0, size, first=first):
                            at = pl.ds(first + r0, size)
                            value = own(c, me, first + r0, size)
                            for way, w, h0 in ways:
                                if k > 1 or h0 == first:
                                    value = value + got[w, at, :].astype(F32)
                            total(c, first + r0, size, value)

                        rows_loop(half, lanes, add)
                self._left(c, site, like)

            steps.append(Step(start, finish))
        return steps

    def _chain_gather(self, axis, rows, block, like):
        n = DIMS[axis]
        k = n // 2
        half = rows // 2
        ways = ((1, 0), (-1, half))
        steps = []
        for s in range(1, k + 1):
            site = self._site()

            def start(c, s=s, site=site):
                for way, h0 in ways:
                    t = self.torus.shifted(axis, -way * (s - 1))
                    ref = block(c, t, h0, half) if s == k else block(c, t, 0, rows)
                    self._copy(c, site, ref, ref, axis, way)

            def finish(c, s=s, site=site):
                both = like(c, 1 if s == k else 2)
                self._arrived(c, site, both)
                self._left(c, site, both)

            steps.append(Step(start, finish))
        return steps

    def _direct(self, axis, rows, lanes, send_ref, own, rx, total):
        n = DIMS[axis]
        site = self._site()

        def start(c):
            for by in range(1, n):
                t = self.torus.shifted(axis, by)
                self._copy(c, site, send_ref(c, t), rx(c).at[by - 1], axis, by)

        def finish(c):
            self._arrived(c, site, rx(c))

            def add(r0, size):
                value = own(c, r0, size)
                for i in range(n - 1):
                    value = value + rx(c)[i, pl.ds(r0, size), :].astype(F32)
                total(c, r0, size, value)

            rows_loop(rows, lanes, add)
            self._left(c, site, rx(c))

        return [Step(start, finish)]

    def _direct_gather(self, axis, mine, like):
        n = DIMS[axis]
        site = self._site()

        def start(c):
            for by in range(1, n):
                self._copy(c, site, mine(c), mine(c), axis, by)

        def finish(c):
            self._arrived(c, site, like(c))
            self._left(c, site, like(c))

        return [Step(start, finish)]

    def _steps(self):
        a1, a2, a3 = self.order
        rows1, lanes2, rows3 = self.rows1, self.lanes2, self.rows3
        at = [self.torus.at[a] for a in self.order]
        chunk = self.chunk

        def block1(c, t, r0, n):
            return chunk(c).at[ds(t * rows1 + r0, n, 16), :]

        def own1(c, t, r0, n):
            return chunk(c)[ds(t * rows1 + r0, n, 16), :].astype(F32)

        def total1(c, r0, n, value):
            at_ = ds(r0, n, 16)
            self.p32[at_, :] = value
            self.pb[at_, :] = value.astype(BF16)

        steps = self._chain(a1, rows1, BLOCK, block1, own1, lambda c, s: self.rx1.at[lax.rem(c, SLOTS), s], total1)

        def own2(c, t, r0, n):
            return self.p32[ds(r0, n, 16), ds(t * lanes2, lanes2)]

        def total2(c, r0, n, value):
            at_ = ds(r0, n, 16)
            self.r32[at_, :] = value
            self.rb[at_, :] = value.astype(BF16)

        if self.chained:
            steps += self._chain(
                a2,
                rows1,
                lanes2,
                lambda c, t, r0, n: self.pb.at[ds(r0, n, 16), ds(t * lanes2, lanes2)],
                own2,
                lambda c, s: self.rx2.at[lax.rem(c, SLOTS), s],
                total2,
            )
        else:
            steps += self._direct(
                a2,
                rows1,
                lanes2,
                lambda c, t: self.pb.at[:, ds(t * lanes2, lanes2)],
                lambda c, r0, n: own2(c, at[1], r0, n),
                lambda c: self.rx2.at[lax.rem(c, SLOTS)],
                total2,
            )

        def final(c):
            return chunk(c).at[ds(at[0] * rows1 + at[2] * rows3, rows3, 16), ds(at[1] * lanes2, lanes2)]

        def total3(c, r0, n, value):
            final(c)[ds(r0, n, 16), :] = value.astype(BF16)

        steps += self._direct(
            a3,
            rows3,
            lanes2,
            lambda c, t: self.rb.at[ds(t * rows3, rows3, 16), :],
            lambda c, r0, n: self.r32[ds(at[2] * rows3 + r0, n, 16), :],
            lambda c: self.rx3.at[lax.rem(c, SLOTS)],
            total3,
        )
        steps += self._direct_gather(a3, final, lambda c: self.rx3.at[lax.rem(c, SLOTS)])

        def block2(c, t, r0, n):
            return chunk(c).at[ds(at[0] * rows1 + r0, n, 16), ds(t * lanes2, lanes2)]

        if self.chained:
            steps += self._chain_gather(a2, rows1, block2, lambda c, n: chunk(c).at[pl.ds(0, rows1), pl.ds(0, n * lanes2)])
        else:
            steps += self._direct_gather(a2, lambda c: block2(c, at[1], 0, rows1), lambda c: self.rx2.at[lax.rem(c, SLOTS)])
        steps += self._chain_gather(a1, rows1, block1, lambda c, n: chunk(c).at[pl.ds(0, n * rows1), :])
        return steps

    @staticmethod
    def scratch(order, chained, chunks):
        n1, n2, n3 = (DIMS[a] for a in order)
        rows1, lanes2 = BLOCK // n1, BLOCK // n2
        rx2 = (chunks, n2 // 2, 2, rows1, lanes2) if chained else (chunks, n2 - 1, rows1, lanes2)
        return [
            pltpu.VMEM((chunks, n1 // 2, 2, rows1, BLOCK), BF16),
            pltpu.VMEM(rx2, BF16),
            pltpu.VMEM((chunks, n3 - 1, rows1 // n3, lanes2), BF16),
            pltpu.VMEM((rows1, BLOCK), F32),
            pltpu.VMEM((rows1, BLOCK), BF16),
            pltpu.VMEM((rows1, lanes2), F32),
            pltpu.VMEM((rows1, lanes2), BF16),
        ]

    @staticmethod
    def n_sites(order, chained):
        k1, k2 = DIMS[order[0]] // 2, DIMS[order[1]] // 2
        return 2 * k1 + (2 * k2 if chained else 2) + 2


DOWN, GATE, UP = range(3)
COLOURS = (((0, 1, 2), True), ((1, 0, 2), True), ((2, 0, 1), False))


def dot(a, b, dims=(((1,), (0,)), ((), ()))):
    return lax.dot_general(a, b, dims, preferred_element_type=F32)


def inverse_rms(wide):
    return lax.rsqrt(jnp.mean(wide * wide, -1, keepdims=True) + 1e-6)


def normed(h):
    wide = h.astype(F32)
    return (wide * inverse_rms(wide)).astype(BF16)


def sigmoid(x):
    return 0.5 * jnp.tanh(0.5 * x) + 0.5


def tiles(rows, size, body):
    def one(i, _):
        body(pl.ds(pl.multiple_of(i * size, size), size))
        return 0

    lax.fori_loop(0, rows // size, one, 0)


class Compute:
    def __init__(self, weights, states, dh, a, by, da):
        self.weights = weights
        self.states = states
        self.dh = dh
        self.a = a
        self.by = by
        self.da = da

    def forward(self, number):
        rows, blocks = self.a.shape[0], self.weights.shape[2]

        def body(at):
            h = self.states[number, at, :]
            a = normed(h)
            out = None
            for block in range(blocks):
                gate = dot(a, self.weights[GATE, number, block])
                up = dot(a, self.weights[UP, number, block])
                part = dot((gate * sigmoid(gate) * up).astype(BF16), self.weights[DOWN, number, block])
                out = part if out is None else out + part
            h = h + out.astype(BF16)
            self.states[number + 1, at, :] = h
            self.a[at, :] = normed(h)

        tiles(rows, min(TILE, rows), body)

    def back(self, number, block, tile):
        size = self.a.shape[0] // 4
        at = pl.ds(tile * size, size)
        a = self.a[at, :]
        gate = dot(a, self.weights[GATE, number, block])
        up = dot(a, self.weights[UP, number, block])
        by = dot(self.dh[at, :], self.weights[DOWN, number, block], NT).astype(BF16).astype(F32)
        s = sigmoid(gate)
        silu = gate * s
        self.by[DOWN, at, :] = (silu * up).astype(BF16)
        self.by[GATE, at, :] = (by * up * (s + silu * (1.0 - s))).astype(BF16)
        self.by[UP, at, :] = (by * silu).astype(BF16)

    def gradient(self, which, into):
        if which == DOWN:
            into[...] = dot(self.by[DOWN], self.dh[...], TN).astype(BF16)
        else:
            into[...] = dot(self.a[...], self.by[which], TN).astype(BF16)

    def inputs(self, number, block, tile):
        size = self.a.shape[0] // 2
        at = pl.ds(tile * size, size)
        part = dot(self.by[GATE, at, :], self.weights[GATE, number, block], NT)
        part = part + dot(self.by[UP, at, :], self.weights[UP, number, block], NT)
        self.da[at, :] = jnp.where(block == 0, 0.0, self.da[at, :]) + part

    def below(self, number):
        rows = self.a.shape[0]

        def body(at):
            wide = self.states[number, at, :].astype(F32)
            by = self.da[at, :].astype(BF16).astype(F32)
            scale = inverse_rms(wide)
            by = by * scale - wide * (scale * scale * scale * jnp.mean(by * wide, -1, keepdims=True))
            self.dh[at, :] = self.dh[at, :] + by.astype(BF16)
            self.a[at, :] = normed(self.states[number - 1, at, :])

        tiles(rows, min(256, rows), body)


def block_at(arrays, which, number, j, r0=0, n=BLOCK):
    if which == DOWN:
        return arrays[2].at[number, ds(j * BLOCK + r0, n), :]
    return arrays[which - 1].at[number, ds(r0, n), ds(j * BLOCK, BLOCK)]


def train_kernel(x, dy, *refs):
    weights, moments, (g, w, kept), refs = refs[:3], (refs[3:6], refs[6:9]), refs[9:12], refs[12:]
    (states, dh, a, by, da), scratch = refs[:5], refs[5:]
    scratch, (send_sems, recv_sems, in_sems) = scratch[:-3], scratch[-3:]
    _, layers, blocks, _, _ = w.shape
    chunks = layers * blocks
    assert layers == 2
    torus = Torus()
    wait_barrier = torus.barrier()
    early = [(x.at[0], states.at[0])]
    early += [(block_at(weights, which, 0, j), w.at[which, 0, j]) for j in range(blocks) for which in (GATE, UP, DOWN)]
    late = [(block_at(weights, which, 1, j), w.at[which, 1, j]) for j in range(blocks) for which in (GATE, UP, DOWN)]
    late.append((dy.at[0], dh))
    idle = [
        (block_at(moments[k], which, layers - 1, j), kept.at[k, which, j])
        for k in range(2)
        for which in range(3)
        for j in range(blocks)
    ]

    def copies(pairs, group):
        return [pltpu.make_async_copy(src, dst, in_sems.at[group, i]) for i, (src, dst) in enumerate(pairs)]

    early, late, idle = (copies(pairs, group) for group, pairs in enumerate((early, late, idle)))
    for copy in (*early, *late):
        copy.start()
    compute = Compute(w, states, dh, a, by, da)
    for copy in early:
        copy.wait()
    compute.forward(0)
    for copy in late:
        copy.wait()
    for copy in idle:
        copy.start()
    wait_barrier()

    sites, exchanges = [0], []
    for k, (order, chained) in enumerate(COLOURS):
        rx, temporary = scratch[7 * k : 7 * k + 3], scratch[7 * k + 3 : 7 * k + 7]
        exchanges.append(Exchange(torus, order, chained, lambda c, k=k: g.at[c, k], rx, *temporary, (send_sems, recv_sems), sites))

    def stage(c, k, s):
        steps = exchanges[k].steps
        if s:
            steps[s - 1].finish(c)
        if s < len(steps):
            steps[s].start(c)

    def work(name, c):
        number, block = layers - 1 - lax.div(c, blocks), lax.rem(c, blocks)
        if name == "below":

            @pl.when((c > 0) & (c < chunks) & (block == 0))
            def _():
                compute.below(number + 1)

            return
        what, _, tile = name.partition(" ")

        @pl.when(c < (chunks - blocks if what == "inputs" else chunks))
        def _():
            if what == "back":
                compute.back(number, block, int(tile))
            elif what == "inputs":
                compute.inputs(number, block, int(tile))
            else:
                which = ("down", "gate", "up").index(what)
                compute.gradient(which, g.at[c, which])

    lags = [item[2] for item in PERIOD if not isinstance(item, str)]

    def body(period, _):
        i = 0
        while i < len(PERIOD):
            if isinstance(PERIOD[i], str):
                work(PERIOD[i], period)
                i += 1
                continue
            j = i
            while j < len(PERIOD) and not isinstance(PERIOD[j], str) and PERIOD[j][2] == PERIOD[i][2]:
                j += 1
            c = period - PERIOD[i][2]

            @pl.when((c >= 0) & (c < chunks))
            def _(c=c, group=PERIOD[i:j]):
                for k, s, _ in group:
                    stage(c, k, s)

            i = j
        return 0

    lax.fori_loop(0, chunks + max(lags), body, 0)
    for copy in idle:
        copy.wait()


def gradients(x, dy, weights, moments):
    gate, up, down = weights
    layers, d, ff = gate.shape
    tokens = x.shape[1]
    chunks = layers * ff // BLOCK
    scratch = [
        pltpu.VMEM((layers, tokens, d), BF16),
        pltpu.VMEM((tokens, d), BF16),
        pltpu.VMEM((tokens, d), BF16),
        pltpu.VMEM((3, tokens, BLOCK), BF16),
        pltpu.VMEM((tokens, d), F32),
    ]
    n_sites = 0
    for order, chained in COLOURS:
        scratch += Exchange.scratch(order, chained, SLOTS)
        n_sites += Exchange.n_sites(order, chained)
    scratch += [pltpu.SemaphoreType.DMA((SLOTS, n_sites))] * 2 + [pltpu.SemaphoreType.DMA((3, 6 * ff // BLOCK))]
    out = [
        pltpu.VMEM((chunks, 3, BLOCK, BLOCK), BF16),
        pltpu.VMEM((3, layers, ff // BLOCK, BLOCK, BLOCK), BF16),
        pltpu.VMEM((2, 3, ff // BLOCK, BLOCK, BLOCK), F32),
    ]
    return pl.pallas_call(
        train_kernel,
        out_shape=out,
        in_specs=[pl.BlockSpec(memory_space=pltpu.HBM)] * 11,
        out_specs=[pl.BlockSpec(memory_space=pltpu.VMEM)] * len(out),
        scratch_shapes=scratch,
        compiler_params=pltpu.CompilerParams(collective_id=0, has_side_effects=True, vmem_limit_bytes=VMEM_LIMIT),
        name="gradients",
    )(x, dy, *weights, *moments)


def adamw(w, m, v, g):
    m = 0.9 * m + 0.1 * g
    v = 0.95 * v + 0.05 * g * g
    step = m * lax.rsqrt(v + 1e-8) + 0.1 * w
    return (w - 0.02 * step).astype(BF16), m, v


def adamw_kernel(g, w, kept, *refs):
    moments, new, refs = (refs[:3], refs[3:6]), (refs[6:9], refs[9:12], refs[12:15]), refs[15:]
    first, *staged, in_sems, out_sems = refs
    _, layers, blocks, _, _ = w.shape
    parts = BLOCK // PIECE

    def load(which, j):
        return [
            pltpu.make_async_copy(block_at(moments[k], which, 0, j), first.at[k, which, j], in_sems.at[k, which, j])
            for k in range(2)
        ]

    def save(number, slot, which, j, r0):
        return [
            pltpu.make_async_copy(staged[k].at[number, slot], block_at(new[k], which, number, j, r0, PIECE), out_sems.at[number, slot, k])
            for k in range(3)
        ]

    for which in range(3):
        for j in range(blocks):
            for copy in load(which, j):
                copy.start()

    for which in range(3):

        def one(i, _, which=which):
            j, r = lax.div(i, parts), lax.rem(i, parts)
            slot = lax.rem(i, OUTPUTS)

            @pl.when(r == 0)
            def _():
                for copy in load(which, j):
                    copy.wait()

            for number in reversed(range(layers)):

                @pl.when(which * blocks * parts + i >= OUTPUTS)
                def _(number=number):
                    for copy in save(number, slot, which, j, r * PIECE):
                        copy.wait()

                moment = kept if number else first
                for r0 in range(0, PIECE, STRIP):
                    rows = ds(r * PIECE + r0, STRIP)
                    grad = g[(layers - 1 - number) * blocks + j, which, rows, :].astype(F32)
                    now = adamw(w[which, number, j, rows, :].astype(F32), moment[0, which, j, rows, :], moment[1, which, j, rows, :], grad)
                    for k in range(3):
                        staged[k][number, slot, pl.ds(r0, STRIP), :] = now[k]
                for copy in save(number, slot, which, j, r * PIECE):
                    copy.start()
            return 0

        lax.fori_loop(0, blocks * parts, one, 0)
    for slot in range(OUTPUTS):
        for number in range(layers):
            for copy in save(number, slot, DOWN, 0, 0):
                copy.wait()


def update(g, w, kept, weights, moments):
    _, layers, blocks, _, _ = w.shape
    vmem, hbm = pl.BlockSpec(memory_space=pltpu.VMEM), pl.BlockSpec(memory_space=pltpu.HBM)
    return pl.pallas_call(
        adamw_kernel,
        out_shape=[jax.ShapeDtypeStruct(a.shape, BF16) for a in weights] + [jax.ShapeDtypeStruct(a.shape, F32) for a in moments],
        in_specs=[vmem] * 3 + [hbm] * 6,
        out_specs=[hbm] * 9,
        scratch_shapes=[
            pltpu.VMEM((2, 3, blocks, BLOCK, BLOCK), F32),
            *(pltpu.VMEM((layers, OUTPUTS, PIECE, BLOCK), dtype) for dtype in (BF16, F32, F32)),
            pltpu.SemaphoreType.DMA((2, 3, blocks)),
            pltpu.SemaphoreType.DMA((layers, OUTPUTS, 3)),
        ],
        compiler_params=pltpu.CompilerParams(vmem_limit_bytes=UPDATE_LIMIT),
        name="update",
    )(g, w, kept, *moments)


def solution(mesh):
    def step(x, dy, *arrays):
        weights, moments = arrays[:3], arrays[3:]
        there = gradients(x, dy, weights, moments)
        there = [pltpu.with_memory_space_constraint(a, pltpu.VMEM) for a in there]
        moments = [pltpu.with_memory_space_constraint(a, pltpu.HBM) for a in moments]
        return tuple(update(*there, weights, moments))

    return jax.shard_map(
        step,
        mesh=mesh,
        in_specs=(P(("rep", "dp"), None, None),) * 2 + (P(None, None, None),) * 9,
        out_specs=(P("rep", None, None),) * 9,
        check_vma=False,
    )
```

time: 216 us -> 182 us (0.84)
  other arithmetic: 34.4 us -> 0 us
    convert_element_type x2 -> x0, other arithmetic: 34.4 us -> none  [adamw(): return ((w - 0.02 * step).astype(jnp.bfloat16), m, v)]
    pallas_call x1 -> x2, Pallas kernels: 181 us -> 181 us  [the longest x1 160 us: gradients(): pl.pallas_call(train_kernel, out_shape=out, in_specs=[pl.BlockSpec(memory...]
where the time goes in v1:
time: 182 us; the launch traced here: 181 us
  Pallas kernels  181 us (99%)
    pallas_call x1, Pallas kernels, gradients(): pl.pallas_call(train_kernel, out_shape=out, in_specs=[pl.BlockSpec(memory...  160 us
    pallas_call x1, Pallas kernels, update(): pl.pallas_call(adamw_kernel, out_shape=[jax.ShapeDtypeStruct(a.shape, BF1...  21 us

profile of v1, /device:TPU:2, one launch (start us, length us, event | category | flops | bytes accessed | tf_op | source)
XLA Modules:
  0.0 181.4 jit_solution(15366049371423802245)
XLA Ops:
  0.6 159.8 %gradients.1 = (bf16[6,3,512,512]{3,2,1,0:T(8,128)(2,1)S(1)}, bf16[3,2,3,512,512]{4,3,2,1,0:T(8,128)(2,1)S(1)}, f32[2,3,3,512,512]{4,3,2,1,0:T(8,128)S(1)}) custom-call(bf16[1,2048,512]{2,1,0:T(8,128)(2,1)} %x.1, bf16[1,2048,512]{2,1,0:T(8,128)(2,1)} %dy.1, bf16[2,512,1536]{2,1,0:T(8,128)(2,1)} %refs_0_.2, bf16[2,512,1536]{2,1,0:T(8,128)(2,1)} %refs_1_.2, ...), custom_call_target="tpu_custom_call" | custom-call | tf_op jit(solution)/shard_map/gradients/pallas_call | solution.py:555
  160.5 21.0 %update.1 = (bf16[2,512,1536]{2,1,0:T(8,128)(2,1)}, bf16[2,512,1536]{2,1,0:T(8,128)(2,1)}, bf16[2,1536,512]{2,1,0:T(8,128)(2,1)}, f32[2,512,1536]{2,1,0:T(8,128)...) custom-call(bf16[6,3,512,512]{3,2,1,0:T(8,128)(2,1)S(1)} %get-tuple-, ...), custom_call_target="tpu_custom_call" | custom-call | tf_op jit(solution)/shard_map/update/pallas_call | solution.py:635

commit v2 on v1

--- a/solution.py
+++ b/solution.py
@@ -17,25 +17,25 @@
 OUTPUTS = 4
 PERIOD = (
     "below",
-    (2, 8, 3), (0, 7, 3),
+    (1, 3, 2), (0, 1, 1), (1, 7, 4), (1, 9, 5), (0, 8, 4),
     "back 0",
-    (2, 5, 2), (1, 1, 1), (0, 9, 4), (1, 7, 3), (2, 2, 1),
+    (0, 4, 2),
     "back 1",
-    (0, 2, 1), (1, 9, 4), (2, 11, 4), (0, 5, 2),
+    (2, 2, 1), (0, 6, 3), (2, 11, 5), (2, 5, 2),
     "back 2",
-    (0, 8, 3), (2, 6, 2), (1, 5, 2), (1, 2, 1), (2, 9, 3),
+    (1, 4, 2), (2, 8, 3),
     "back 3",
-    (2, 3, 1), (0, 3, 1), (1, 8, 3),
+    (0, 2, 1), (0, 10, 5), (1, 1, 1),
     "up",
-    (2, 7, 2), (0, 10, 4), (1, 10, 4), (2, 12, 4), (2, 0, 0),
+    (2, 0, 0), (2, 3, 1), (2, 6, 2), (1, 8, 4), (1, 6, 3), (0, 7, 3),
     "down",
-    (0, 0, 0), (2, 10, 3), (0, 6, 2), (0, 4, 1), (1, 3, 1), (2, 4, 1),
+    (0, 0, 0), (0, 5, 2), (0, 3, 1), (2, 10, 4),
     "gate",
-    (1, 0, 0), (2, 1, 0),
+    (1, 2, 1), (2, 12, 5), (0, 9, 4), (1, 5, 2),
     "inputs 0",
-    (1, 6, 2),
+    (1, 0, 0), (2, 4, 1), (2, 1, 0), (2, 9, 3),
     "inputs 1",
-    (0, 1, 0), (1, 4, 1),
+    (2, 7, 2), (1, 10, 5),
 )
 VMEM_LIMIT = UPDATE_LIMIT = 29_200_000
 TN = (((0,), (0,)), ((), ()))
@@ -376,12 +376,16 @@
         def body(at):
             h = self.states[number, at, :]
             a = normed(h)
+            for block in range(blocks):
+                for first in range(0, BLOCK, BLOCK // 2):
+                    part = pl.ds(first, BLOCK // 2)
+                    gate = dot(a, self.weights[GATE, number, block, :, part])
+                    up = dot(a, self.weights[UP, number, block, :, part])
+                    self.by[block, at, part] = (gate * sigmoid(gate) * up).astype(BF16)
             out = None
             for block in range(blocks):
-                gate = dot(a, self.weights[GATE, number, block])
-                up = dot(a, self.weights[UP, number, block])
-                part = dot((gate * sigmoid(gate) * up).astype(BF16), self.weights[DOWN, number, block])
-                out = part if out is None else out + part
+                more = dot(self.by[block, at, :], self.weights[DOWN, number, block])
+                out = more if out is None else out + more
             h = h + out.astype(BF16)
             self.states[number + 1, at, :] = h
             self.a[at, :] = normed(h)
@@ -391,15 +395,17 @@
     def back(self, number, block, tile):
         size = self.a.shape[0] // 4
         at = pl.ds(tile * size, size)
-        a = self.a[at, :]
-        gate = dot(a, self.weights[GATE, number, block])
-        up = dot(a, self.weights[UP, number, block])
-        by = dot(self.dh[at, :], self.weights[DOWN, number, block], NT).astype(BF16).astype(F32)
-        s = sigmoid(gate)
-        silu = gate * s
-        self.by[DOWN, at, :] = (silu * up).astype(BF16)
-        self.by[GATE, at, :] = (by * up * (s + silu * (1.0 - s))).astype(BF16)
-        self.by[UP, at, :] = (by * silu).astype(BF16)
+        for first in range(0, BLOCK, BLOCK // 2):
+            part = pl.ds(first, BLOCK // 2)
+            a = self.a[at, :]
+            gate = dot(a, self.weights[GATE, number, block, :, part])
+            up = dot(a, self.weights[UP, number, block, :, part])
+            by = dot(self.dh[at, :], self.weights[DOWN, number, block, part, :], NT).astype(BF16).astype(F32)
+            s = sigmoid(gate)
+            silu = gate * s
+            self.by[DOWN, at, part] = (silu * up).astype(BF16)
+            self.by[GATE, at, part] = (by * up * (s + silu * (1.0 - s))).astype(BF16)
+            self.by[UP, at, part] = (by * silu).astype(BF16)
 
     def gradient(self, which, into):
         if which == DOWN:

time: 182 us -> 170 us (0.934)
  Pallas kernels: 181 us -> 169 us
    pallas_call x1, Pallas kernels: 160 us -> 148 us  [gradients(): pl.pallas_call(train_kernel, out_shape=out, in_specs=[pl.BlockSpec(memory...]
where the time goes in v2:
time: 170 us
  Pallas kernels  169 us (99%)
    pallas_call x1, Pallas kernels, gradients(): pl.pallas_call(train_kernel, out_shape=out, in_specs=[pl.BlockSpec(memory...  148 us
    pallas_call x1, Pallas kernels, update(): pl.pallas_call(adamw_kernel, out_shape=[jax.ShapeDtypeStruct(a.shape, BF1...  21 us

profile of v2, /device:TPU:2, one launch (start us, length us, event | category | flops | bytes accessed | tf_op | source)
XLA Modules:
  0.0 169.7 jit_solution(5933938460527154756)
XLA Ops:
  0.6 148.1 %gradients.1 = (bf16[6,3,512,512]{3,2,1,0:T(8,128)(2,1)S(1)}, bf16[3,2,3,512,512]{4,3,2,1,0:T(8,128)(2,1)S(1)}, f32[2,3,3,512,512]{4,3,2,1,0:T(8,128)S(1)}) custom-call(bf16[1,2048,512]{2,1,0:T(8,128)(2,1)} %x.1, bf16[1,2048,512]{2,1,0:T(8,128)(2,1)} %dy.1, bf16[2,512,1536]{2,1,0:T(8,128)(2,1)} %refs_0_.2, bf16[2,512,1536]{2,1,0:T(8,128)(2,1)} %refs_1_.2, ...), custom_call_target="tpu_custom_call" | custom-call | tf_op jit(solution)/shard_map/gradients/pallas_call | solution.py:561
  148.8 21.0 %update.1 = (bf16[2,512,1536]{2,1,0:T(8,128)(2,1)}, bf16[2,512,1536]{2,1,0:T(8,128)(2,1)}, bf16[2,1536,512]{2,1,0:T(8,128)(2,1)}, f32[2,512,1536]{2,1,0:T(8,128)...) custom-call(bf16[6,3,512,512]{3,2,1,0:T(8,128)(2,1)S(1)} %get-tuple-, ...), custom_call_target="tpu_custom_call" | custom-call | tf_op jit(solution)/shard_map/update/pallas_call | solution.py:641

commit v3 on v2

--- a/solution.py
+++ b/solution.py
@@ -16,26 +16,24 @@
 SLOTS = 3
 OUTPUTS = 4
 PERIOD = (
-    "below",
-    (1, 3, 2), (0, 1, 1), (1, 7, 4), (1, 9, 5), (0, 8, 4),
     "back 0",
-    (0, 4, 2),
+    (0, 4, 2), (1, 7, 4), (0, 1, 1), (0, 9, 5),
     "back 1",
-    (2, 2, 1), (0, 6, 3), (2, 11, 5), (2, 5, 2),
+    (2, 2, 1), (2, 5, 2), (1, 9, 5), (0, 6, 3),
     "back 2",
-    (1, 4, 2), (2, 8, 3),
+    (1, 4, 2), (2, 11, 5),
     "back 3",
-    (0, 2, 1), (0, 10, 5), (1, 1, 1),
+    (1, 2, 1), (0, 8, 4), (2, 8, 3),
     "up",
-    (2, 0, 0), (2, 3, 1), (2, 6, 2), (1, 8, 4), (1, 6, 3), (0, 7, 3),
+    (0, 2, 1), (2, 0, 0), (1, 6, 3), (2, 3, 1), (2, 6, 2),
+    "gate",
+    (1, 0, 0), (0, 5, 2),
     "down",
-    (0, 0, 0), (0, 5, 2), (0, 3, 1), (2, 10, 4),
-    "gate",
-    (1, 2, 1), (2, 12, 5), (0, 9, 4), (1, 5, 2),
+    (1, 8, 4), (1, 5, 2), (2, 10, 4), (0, 0, 0),
     "inputs 0",
-    (1, 0, 0), (2, 4, 1), (2, 1, 0), (2, 9, 3),
+    (0, 3, 1), (2, 12, 5), (2, 1, 0), (1, 10, 5), (2, 4, 1), (2, 7, 2),
     "inputs 1",
-    (2, 7, 2), (1, 10, 5),
+    (2, 9, 3), (1, 3, 1), (0, 7, 3), (0, 10, 5), (1, 1, 0),
 )
 VMEM_LIMIT = UPDATE_LIMIT = 29_200_000
 TN = (((0,), (0,)), ((), ()))
@@ -84,11 +82,11 @@
 def rows_loop(rows, lanes, body):
     size = min(rows, 32 * 1024 // lanes)
     for r0 in range(0, rows, size):
-        body(r0, size)
+        body(r0, min(size, rows - r0))
 
 
 class Exchange:
-    def __init__(self, torus, order, chained, chunk, rx, p32, pb, r32, rb, sems, sites):
+    def __init__(self, torus, order, chained, far, chunk, rx, p32, pb, r32, rb, sems, sites):
         self.torus, self.order, self.chained = torus, order, chained
         self.chunk = chunk
         self.rx1, self.rx2, self.rx3 = rx
@@ -97,6 +95,7 @@
         self.sites = sites
         n1, n2, n3 = (DIMS[a] for a in order)
         self.rows1 = BLOCK // n1
+        self.far = int(self.rows1 * far) // 16 * 16
         self.lanes2 = BLOCK // n2
         self.rows3 = self.rows1 // n3
         self.steps = self._steps()
@@ -110,91 +109,97 @@
         pltpu.make_async_remote_copy(
             src_ref=src,
             dst_ref=dst,
-            send_sem=self.send_sems.at[lax.rem(c, SLOTS), site],
+            send_sem=self.send_sems.at[c],
             recv_sem=self.recv_sems.at[lax.rem(c, SLOTS), site],
             device_id=self.torus.device(axis, by),
             device_id_type=MESH,
         ).start()
 
+    @staticmethod
+    def _blocks(ref):
+        def rx(c, i, n=None):
+            return ref.at[lax.rem(c, SLOTS), i if n is None else pl.ds(i, n)]
+
+        return rx
+
     def _arrived(self, c, site, like):
         pltpu.make_async_copy(like, like, self.recv_sems.at[lax.rem(c, SLOTS), site]).wait()
 
-    def _left(self, c, site, like):
-        pltpu.make_async_copy(like, like, self.send_sems.at[lax.rem(c, SLOTS), site]).wait()
-
-    def _chain(self, axis, rows, lanes, send_ref, own, rx, total):
-        n = DIMS[axis]
-        k = n // 2
-        half = rows // 2
-        ways = ((1, 0, 0), (-1, 1, half))
+    def _left(self, c, like):
+        pltpu.make_async_copy(like, like, self.send_sems.at[c]).wait()
+
+    def _chain(self, axis, rows, far, lanes, send_ref, own, rx, total):
+        k = DIMS[axis] // 2
+        ways = ((1, 0, (0, far), (far, rows - far)), (-1, 1, (far, rows - far), (0, far)))
+
+        def got(c, s, w):
+            return rx(c, 0 if s == 1 else 2 * s - 3 + w)
+
         steps = []
         for s in range(1, k + 1):
             site = self._site()
 
             def start(c, s=s, site=site):
-                for way, w, h0 in ways:
+                for way, w, mine, others in ways:
                     t = self.torus.shifted(axis, way * (k + 1 - s))
-                    dst = rx(c, s - 1).at[w]
+                    dst = got(c, s, w)
                     if s == 1:
-                        self._copy(c, site, send_ref(c, t, h0, half), dst.at[ds(h0, half), :], axis, way)
+                        self._copy(c, site, send_ref(c, t, *mine), dst.at[ds(*mine, 16), :], axis, way)
                     elif s == 2:
-                        o0 = half - h0
-                        self._copy(c, site, rx(c, 0).at[w, ds(h0, half), :], dst.at[ds(h0, half), :], axis, way)
-                        self._copy(c, site, send_ref(c, t, o0, half), dst.at[ds(o0, half), :], axis, way)
+                        self._copy(c, site, got(c, 1, w).at[ds(*mine, 16), :], dst.at[ds(*mine, 16), :], axis, way)
+                        self._copy(c, site, send_ref(c, t, *others), dst.at[ds(*others, 16), :], axis, way)
                     else:
-                        self._copy(c, site, rx(c, s - 2).at[w], dst, axis, way)
+                        self._copy(c, site, got(c, s - 1, w), dst, axis, way)
 
             def finish(c, s=s, site=site):
-                got = rx(c, s - 1)
-                like = got.at[0] if s == 1 else got
+                like = rx(c, 0) if s == 1 else rx(c, 2 * s - 3, 2)
                 self._arrived(c, site, like)
                 if s < k:
-                    for way, w, h0 in ways:
+                    for way, w, mine, _ in ways:
                         t = self.torus.shifted(axis, way * (k - s))
-                        first, count = (h0, half) if s == 1 else (0, rows)
-
-                        def add(r0, size, w=w, t=t, first=first):
+                        first, count = mine if s == 1 else (0, rows)
+                        here = got(c, s, w)
+
+                        def add(r0, size, here=here, t=t, first=first):
                             at = pl.ds(first + r0, size)
-                            got[w, at, :] = (got[w, at, :].astype(F32) + own(c, t, first + r0, size)).astype(BF16)
+                            here[at, :] = (here[at, :].astype(F32) + own(c, t, first + r0, size)).astype(BF16)
 
                         rows_loop(count, lanes, add)
                 else:
                     me = self.torus.shifted(axis, 0)
-                    for first in (0, half):
-
-                        def add(r0, size, first=first):
+                    for _, here, (first, count), _ in ways:
+
+                        def add(r0, size, here=here, first=first):
                             at = pl.ds(first + r0, size)
                             value = own(c, me, first + r0, size)
-                            for way, w, h0 in ways:
-                                if k > 1 or h0 == first:
-                                    value = value + got[w, at, :].astype(F32)
+                            for w in range(2):
+                                if k > 1 or w == here:
+                                    value = value + got(c, s, w)[at, :].astype(F32)
                             total(c, first + r0, size, value)
 
-                        rows_loop(half, lanes, add)
-                self._left(c, site, like)
+                        rows_loop(count, lanes, add)
+                self._left(c, like)
 
             steps.append(Step(start, finish))
         return steps
 
-    def _chain_gather(self, axis, rows, block, like):
-        n = DIMS[axis]
-        k = n // 2
-        half = rows // 2
-        ways = ((1, 0), (-1, half))
+    def _chain_gather(self, axis, rows, far, block, like):
+        k = DIMS[axis] // 2
+        ways = ((1, (0, far)), (-1, (far, rows - far)))
         steps = []
         for s in range(1, k + 1):
             site = self._site()
 
             def start(c, s=s, site=site):
-                for way, h0 in ways:
+                for way, mine in ways:
                     t = self.torus.shifted(axis, -way * (s - 1))
-                    ref = block(c, t, h0, half) if s == k else block(c, t, 0, rows)
+                    ref = block(c, t, *mine) if s == k else block(c, t, 0, rows)
                     self._copy(c, site, ref, ref, axis, way)
 
             def finish(c, s=s, site=site):
                 both = like(c, 1 if s == k else 2)
                 self._arrived(c, site, both)
-                self._left(c, site, both)
+                self._left(c, both)
 
             steps.append(Step(start, finish))
         return steps
@@ -218,7 +223,7 @@
                 total(c, r0, size, value)
 
             rows_loop(rows, lanes, add)
-            self._left(c, site, rx(c))
+            self._left(c, rx(c))
 
         return [Step(start, finish)]
 
@@ -232,7 +237,7 @@
 
         def finish(c):
             self._arrived(c, site, like(c))
-            self._left(c, site, like(c))
+            self._left(c, like(c))
 
         return [Step(start, finish)]
 
@@ -253,7 +258,7 @@
             self.p32[at_, :] = value
             self.pb[at_, :] = value.astype(BF16)
 
-        steps = self._chain(a1, rows1, BLOCK, block1, own1, lambda c, s: self.rx1.at[lax.rem(c, SLOTS), s], total1)
+        steps = self._chain(a1, rows1, self.far, BLOCK, block1, own1, self._blocks(self.rx1), total1)
 
         def own2(c, t, r0, n):
             return self.p32[ds(r0, n, 16), ds(t * lanes2, lanes2)]
@@ -267,10 +272,11 @@
             steps += self._chain(
                 a2,
                 rows1,
+                rows1 // 2,
                 lanes2,
                 lambda c, t, r0, n: self.pb.at[ds(r0, n, 16), ds(t * lanes2, lanes2)],
                 own2,
-                lambda c, s: self.rx2.at[lax.rem(c, SLOTS), s],
+                self._blocks(self.rx2),
                 total2,
             )
         else:
@@ -305,19 +311,19 @@
             return chunk(c).at[ds(at[0] * rows1 + r0, n, 16), ds(t * lanes2, lanes2)]
 
         if self.chained:
-            steps += self._chain_gather(a2, rows1, block2, lambda c, n: chunk(c).at[pl.ds(0, rows1), pl.ds(0, n * lanes2)])
+            steps += self._chain_gather(a2, rows1, rows1 // 2, block2, lambda c, n: chunk(c).at[pl.ds(0, rows1), pl.ds(0, n * lanes2)])
         else:
             steps += self._direct_gather(a2, lambda c: block2(c, at[1], 0, rows1), lambda c: self.rx2.at[lax.rem(c, SLOTS)])
-        steps += self._chain_gather(a1, rows1, block1, lambda c, n: chunk(c).at[pl.ds(0, n * rows1), :])
+        steps += self._chain_gather(a1, rows1, self.far, block1, lambda c, n: chunk(c).at[pl.ds(0, n * rows1), :])
         return steps
 
     @staticmethod
     def scratch(order, chained, chunks):
         n1, n2, n3 = (DIMS[a] for a in order)
         rows1, lanes2 = BLOCK // n1, BLOCK // n2
-        rx2 = (chunks, n2 // 2, 2, rows1, lanes2) if chained else (chunks, n2 - 1, rows1, lanes2)
+        rx2 = (chunks, n2 - 1, rows1, lanes2) if chained else (chunks, n2 - 1, rows1, lanes2)
         return [
-            pltpu.VMEM((chunks, n1 // 2, 2, rows1, BLOCK), BF16),
+            pltpu.VMEM((chunks, n1 - 1, rows1, BLOCK), BF16),
             pltpu.VMEM(rx2, BF16),
             pltpu.VMEM((chunks, n3 - 1, rows1 // n3, lanes2), BF16),
             pltpu.VMEM((rows1, BLOCK), F32),
@@ -333,7 +339,7 @@
 
 
 DOWN, GATE, UP = range(3)
-COLOURS = (((0, 1, 2), True), ((1, 0, 2), True), ((2, 0, 1), False))
+COLOURS = (((0, 1, 2), True, 0.375), ((1, 0, 2), True, 0.5), ((2, 0, 1), False, 0.25))
 
 
 def dot(a, b, dims=(((1,), (0,)), ((), ()))):
@@ -351,14 +357,6 @@
 
 def sigmoid(x):
     return 0.5 * jnp.tanh(0.5 * x) + 0.5
-
-
-def tiles(rows, size, body):
-    def one(i, _):
-        body(pl.ds(pl.multiple_of(i * size, size), size))
-        return 0
-
-    lax.fori_loop(0, rows // size, one, 0)
 
 
 class Compute:
@@ -370,27 +368,38 @@
         self.by = by
         self.da = da
 
-    def forward(self, number):
+    def forward(self, wait):
         rows, blocks = self.a.shape[0], self.weights.shape[2]
-
-        def body(at):
-            h = self.states[number, at, :]
+        size = min(TILE, rows)
+
+        def tile(at, wait):
+            h = self.states[0, at, :]
             a = normed(h)
             for block in range(blocks):
+                wait("in", block)
                 for first in range(0, BLOCK, BLOCK // 2):
                     part = pl.ds(first, BLOCK // 2)
-                    gate = dot(a, self.weights[GATE, number, block, :, part])
-                    up = dot(a, self.weights[UP, number, block, :, part])
+                    gate = dot(a, self.weights[GATE, 0, block, :, part])
+                    up = dot(a, self.weights[UP, 0, block, :, part])
                     self.by[block, at, part] = (gate * sigmoid(gate) * up).astype(BF16)
+            wait("out", 0)
             out = None
             for block in range(blocks):
-                more = dot(self.by[block, at, :], self.weights[DOWN, number, block])
+                more = dot(self.by[block, at, :], self.weights[DOWN, 0, block])
                 out = more if out is None else out + more
             h = h + out.astype(BF16)
-            self.states[number + 1, at, :] = h
+            self.states[1, at, :] = h
             self.a[at, :] = normed(h)
 
-        tiles(rows, min(TILE, rows), body)
+        wait("x", 0)
+        tile(pl.ds(0, size), wait)
+        wait("x", 1)
+
+        def one(i, _):
+            tile(pl.ds(pl.multiple_of(i * size, size), size), lambda what, i: None)
+            return 0
+
+        lax.fori_loop(1, rows // size, one, 0)
 
     def back(self, number, block, tile):
         size = self.a.shape[0] // 4
@@ -413,25 +422,29 @@
         else:
             into[...] = dot(self.a[...], self.by[which], TN).astype(BF16)
 
-    def inputs(self, number, block, tile):
+    def _inputs(self, block, at):
+        part = dot(self.by[GATE, at, :], self.weights[GATE, 1, block], NT)
+        return part + dot(self.by[UP, at, :], self.weights[UP, 1, block], NT)
+
+    def inputs(self, block, tile):
         size = self.a.shape[0] // 2
         at = pl.ds(tile * size, size)
-        part = dot(self.by[GATE, at, :], self.weights[GATE, number, block], NT)
-        part = part + dot(self.by[UP, at, :], self.weights[UP, number, block], NT)
-        self.da[at, :] = jnp.where(block == 0, 0.0, self.da[at, :]) + part
-
-    def below(self, number):
-        rows = self.a.shape[0]
-
-        def body(at):
-            wide = self.states[number, at, :].astype(F32)
-            by = self.da[at, :].astype(BF16).astype(F32)
+        self.da[at, :] = jnp.where(block == 0, 0.0, self.da[at, :]) + self._inputs(block, at)
+
+    def below(self, tile):
+        size = self.a.shape[0] // 8
+
+        def one(i, _):
+            at = pl.ds(pl.multiple_of(i * size, size), size)
+            by = (self.da[at, :] + self._inputs(self.weights.shape[2] - 1, at)).astype(BF16).astype(F32)
+            wide = self.states[1, at, :].astype(F32)
             scale = inverse_rms(wide)
             by = by * scale - wide * (scale * scale * scale * jnp.mean(by * wide, -1, keepdims=True))
             self.dh[at, :] = self.dh[at, :] + by.astype(BF16)
-            self.a[at, :] = normed(self.states[number - 1, at, :])
-
-        tiles(rows, min(256, rows), body)
+            self.a[at, :] = normed(self.states[0, at, :])
+            return 0
+
+        lax.fori_loop(4 * tile, 4 * tile + 4, one, 0)
 
 
 def block_at(arrays, which, number, j, r0=0, n=BLOCK):
@@ -449,37 +462,48 @@
     assert layers == 2
     torus = Torus()
     wait_barrier = torus.barrier()
-    early = [(x.at[0], states.at[0])]
-    early += [(block_at(weights, which, 0, j), w.at[which, 0, j]) for j in range(blocks) for which in (GATE, UP, DOWN)]
-    late = [(block_at(weights, which, 1, j), w.at[which, 1, j]) for j in range(blocks) for which in (GATE, UP, DOWN)]
-    late.append((dy.at[0], dh))
-    idle = [
-        (block_at(moments[k], which, layers - 1, j), kept.at[k, which, j])
-        for k in range(2)
-        for which in range(3)
-        for j in range(blocks)
-    ]
-
-    def copies(pairs, group):
-        return [pltpu.make_async_copy(src, dst, in_sems.at[group, i]) for i, (src, dst) in enumerate(pairs)]
-
-    early, late, idle = (copies(pairs, group) for group, pairs in enumerate((early, late, idle)))
-    for copy in (*early, *late):
-        copy.start()
+    size = min(TILE, dh.shape[0])
+
+    def weight(which, number, j):
+        return block_at(weights, which, number, j), w.at[which, number, j]
+
+    first = x.at[0, pl.ds(0, size)], states.at[0, pl.ds(0, size)]
+    rest = x.at[0, pl.ds(size, x.shape[1] - size)], states.at[0, pl.ds(size, x.shape[1] - size)]
+    groups = {("x", 0): ([first], first[1])}
+    for j in range(blocks):
+        groups["in", j] = [weight(which, 0, j) for which in (GATE, UP)], w.at[pl.ds(GATE, 2), 0, j]
+        if j == 0:
+            groups["out", 0] = [weight(DOWN, 0, i) for i in range(blocks)], w.at[DOWN, 0]
+    groups["x", 1] = [rest], rest[1]
+    groups["late", 0] = [weight(which, 1, j) for j in range(blocks) for which in range(3)], w.at[:, 1]
+    groups["late", 1] = [(dy.at[0], dh)], dh
+    idle = [(block_at(moments[k], i, layers - 1, j), kept.at[k, i, j]) for k in range(2) for i in range(3) for j in range(blocks)]
+    groups["idle", 0] = idle, kept
+    sem_of = {key: i for i, key in enumerate(groups)}
+
+    def begin(key):
+        for src, dst in groups[key][0]:
+            pltpu.make_async_copy(src, dst, in_sems.at[sem_of[key]]).start()
+
+    def wait(*key):
+        like = groups[key][1]
+        pltpu.make_async_copy(like, like, in_sems.at[sem_of[key]]).wait()
+
+    for key in groups:
+        if key[0] != "idle":
+            begin(key)
     compute = Compute(w, states, dh, a, by, da)
-    for copy in early:
-        copy.wait()
-    compute.forward(0)
-    for copy in late:
-        copy.wait()
-    for copy in idle:
-        copy.start()
+    compute.forward(wait)
+    wait("late", 0)
+    wait("late", 1)
+    begin(("idle", 0))
     wait_barrier()
 
     sites, exchanges = [0], []
-    for k, (order, chained) in enumerate(COLOURS):
+    for k, (order, chained, far) in enumerate(COLOURS):
         rx, temporary = scratch[7 * k : 7 * k + 3], scratch[7 * k + 3 : 7 * k + 7]
-        exchanges.append(Exchange(torus, order, chained, lambda c, k=k: g.at[c, k], rx, *temporary, (send_sems, recv_sems), sites))
+        sems = send_sems.at[k], recv_sems
+        exchanges.append(Exchange(torus, order, chained, far, lambda c, k=k: g.at[c, k], rx, *temporary, sems, sites))
 
     def stage(c, k, s):
         steps = exchanges[k].steps
@@ -490,21 +514,23 @@
 
     def work(name, c):
         number, block = layers - 1 - lax.div(c, blocks), lax.rem(c, blocks)
-        if name == "below":
-
-            @pl.when((c > 0) & (c < chunks) & (block == 0))
+        what, _, tile = name.partition(" ")
+        if what == "inputs":
+
+            @pl.when(c < blocks - 1)
             def _():
-                compute.below(number + 1)
+                compute.inputs(block, int(tile))
+
+            @pl.when(c == blocks - 1)
+            def _():
+                compute.below(int(tile))
 
             return
-        what, _, tile = name.partition(" ")
-
-        @pl.when(c < (chunks - blocks if what == "inputs" else chunks))
+
+        @pl.when(c < chunks)
         def _():
             if what == "back":
                 compute.back(number, block, int(tile))
-            elif what == "inputs":
-                compute.inputs(number, block, int(tile))
             else:
                 which = ("down", "gate", "up").index(what)
                 compute.gradient(which, g.at[c, which])
@@ -532,8 +558,7 @@
         return 0
 
     lax.fori_loop(0, chunks + max(lags), body, 0)
-    for copy in idle:
-        copy.wait()
+    wait("idle", 0)
 
 
 def gradients(x, dy, weights, moments):
@@ -549,10 +574,10 @@
         pltpu.VMEM((tokens, d), F32),
     ]
     n_sites = 0
-    for order, chained in COLOURS:
+    for order, chained, _ in COLOURS:
         scratch += Exchange.scratch(order, chained, SLOTS)
         n_sites += Exchange.n_sites(order, chained)
-    scratch += [pltpu.SemaphoreType.DMA((SLOTS, n_sites))] * 2 + [pltpu.SemaphoreType.DMA((3, 6 * ff // BLOCK))]
+    scratch += [pltpu.SemaphoreType.DMA((len(COLOURS), chunks)), pltpu.SemaphoreType.DMA((SLOTS, n_sites)), pltpu.SemaphoreType.DMA((11,))]
     out = [
         pltpu.VMEM((chunks, 3, BLOCK, BLOCK), BF16),
         pltpu.VMEM((3, layers, ff // BLOCK, BLOCK, BLOCK), BF16),

time: 170 us -> 167 us (0.982)
  Pallas kernels: 169 us -> 165 us
    pallas_call x1, Pallas kernels: 148 us -> 144 us  [gradients(): pl.pallas_call(train_kernel, out_shape=out, in_specs=[pl.BlockSpec(memory...]
where the time goes in v3:
time: 167 us; the launch traced here: 166 us
  Pallas kernels  165 us (99%)
    pallas_call x1, Pallas kernels, gradients(): pl.pallas_call(train_kernel, out_shape=out, in_specs=[pl.BlockSpec(memory...  144 us
    pallas_call x1, Pallas kernels, update(): pl.pallas_call(adamw_kernel, out_shape=[jax.ShapeDtypeStruct(a.shape, BF1...  21 us

profile of v3, /device:TPU:2, one launch (start us, length us, event | category | flops | bytes accessed | tf_op | source)
XLA Modules:
  0.0 166.1 jit_solution(8486773914096147756)
XLA Ops:
  0.6 144.3 %gradients.1 = (bf16[6,3,512,512]{3,2,1,0:T(8,128)(2,1)S(1)}, bf16[3,2,3,512,512]{4,3,2,1,0:T(8,128)(2,1)S(1)}, f32[2,3,3,512,512]{4,3,2,1,0:T(8,128)S(1)}) custom-call(bf16[1,2048,512]{2,1,0:T(8,128)(2,1)} %x.1, bf16[1,2048,512]{2,1,0:T(8,128)(2,1)} %dy.1, bf16[2,512,1536]{2,1,0:T(8,128)(2,1)} %refs_0_.2, bf16[2,512,1536]{2,1,0:T(8,128)(2,1)} %refs_1_.2, ...), custom_call_target="tpu_custom_call" | custom-call | tf_op jit(solution)/shard_map/gradients/pallas_call | solution.py:586
  145.0 21.0 %update.1 = (bf16[2,512,1536]{2,1,0:T(8,128)(2,1)}, bf16[2,512,1536]{2,1,0:T(8,128)(2,1)}, bf16[2,1536,512]{2,1,0:T(8,128)(2,1)}, f32[2,512,1536]{2,1,0:T(8,128)...) custom-call(bf16[6,3,512,512]{3,2,1,0:T(8,128)(2,1)S(1)} %get-tuple-, ...), custom_call_target="tpu_custom_call" | custom-call | tf_op jit(solution)/shard_map/update/pallas_call | solution.py:666

commit v4 on v3

--- a/solution.py
+++ b/solution.py
@@ -10,11 +10,12 @@
 MESH = pl.DeviceIdType.MESH
 DIMS = (4, 4, 8)
 BLOCK = 512
-TILE = 512
+LAST = "down"
+KEPT = 14
 PIECE = 128
 STRIP = 32
 SLOTS = 3
-OUTPUTS = 4
+OUTPUTS = 8
 PERIOD = (
     "back 0",
     (0, 4, 2), (1, 7, 4), (0, 1, 1), (0, 9, 5),
@@ -35,7 +36,7 @@
     "inputs 1",
     (2, 9, 3), (1, 3, 1), (0, 7, 3), (0, 10, 5), (1, 1, 0),
 )
-VMEM_LIMIT = UPDATE_LIMIT = 29_200_000
+VMEM_LIMIT = UPDATE_LIMIT = 16_700_000
 TN = (((0,), (0,)), ((), ()))
 NT = (((1,), (1,)), ((), ()))
 BF16, F32 = jnp.bfloat16, jnp.float32
@@ -360,20 +361,23 @@
 
 
 class Compute:
-    def __init__(self, weights, states, dh, a, by, da):
+    def __init__(self, weights, dh, h, a, wide):
         self.weights = weights
-        self.states = states
         self.dh = dh
+        self.h = h
         self.a = a
-        self.by = by
-        self.da = da
-
-    def forward(self, wait):
-        rows, blocks = self.a.shape[0], self.weights.shape[2]
-        size = min(TILE, rows)
-
-        def tile(at, wait):
-            h = self.states[0, at, :]
+        self.wide = wide
+        self.size = a.shape[0] // 4
+
+    def _quarters(self, what, first, count):
+        value = self.wide[4 * what + first : 4 * what + first + count, pl.ds(0, self.size), :]
+        return value.reshape(count * self.size, BLOCK).astype(BF16)
+
+    def forward(self, wait, then):
+        blocks, size = self.weights.shape[2], self.size
+
+        def tile(i, at, wait):
+            h = self.dh[at, :]
             a = normed(h)
             for block in range(blocks):
                 wait("in", block)
@@ -381,29 +385,30 @@
                     part = pl.ds(first, BLOCK // 2)
                     gate = dot(a, self.weights[GATE, 0, block, :, part])
                     up = dot(a, self.weights[UP, 0, block, :, part])
-                    self.by[block, at, part] = (gate * sigmoid(gate) * up).astype(BF16)
+                    self.wide[4 * block + i, pl.ds(0, size), part] = gate * sigmoid(gate) * up
             wait("out", 0)
             out = None
             for block in range(blocks):
-                more = dot(self.by[block, at, :], self.weights[DOWN, 0, block])
+                act = self.wide[4 * block + i, pl.ds(0, size), :].astype(BF16)
+                more = dot(act, self.weights[DOWN, 0, block])
                 out = more if out is None else out + more
             h = h + out.astype(BF16)
-            self.states[1, at, :] = h
+            self.h[at, :] = h
             self.a[at, :] = normed(h)
+            then(at)
 
         wait("x", 0)
-        tile(pl.ds(0, size), wait)
+        tile(0, pl.ds(0, size), wait)
         wait("x", 1)
 
         def one(i, _):
-            tile(pl.ds(pl.multiple_of(i * size, size), size), lambda what, i: None)
+            tile(i, pl.ds(pl.multiple_of(i * size, size), size), lambda what, i: None)
             return 0
 
-        lax.fori_loop(1, rows // size, one, 0)
+        lax.fori_loop(1, 4, one, 0)
 
     def back(self, number, block, tile):
-        size = self.a.shape[0] // 4
-        at = pl.ds(tile * size, size)
+        at, rows = pl.ds(tile * self.size, self.size), pl.ds(0, self.size)
         for first in range(0, BLOCK, BLOCK // 2):
             part = pl.ds(first, BLOCK // 2)
             a = self.a[at, :]
@@ -412,39 +417,51 @@
             by = dot(self.dh[at, :], self.weights[DOWN, number, block, part, :], NT).astype(BF16).astype(F32)
             s = sigmoid(gate)
             silu = gate * s
-            self.by[DOWN, at, part] = (silu * up).astype(BF16)
-            self.by[GATE, at, part] = (by * up * (s + silu * (1.0 - s))).astype(BF16)
-            self.by[UP, at, part] = (by * silu).astype(BF16)
+            self.wide[4 * DOWN + tile, rows, part] = silu * up
+            self.wide[4 * GATE + tile, rows, part] = by * up * (s + silu * (1.0 - s))
+            self.wide[4 * UP + tile, rows, part] = by * silu
 
     def gradient(self, which, into):
-        if which == DOWN:
-            into[...] = dot(self.by[DOWN], self.dh[...], TN).astype(BF16)
-        else:
-            into[...] = dot(self.a[...], self.by[which], TN).astype(BF16)
-
-    def _inputs(self, block, at):
-        part = dot(self.by[GATE, at, :], self.weights[GATE, 1, block], NT)
-        return part + dot(self.by[UP, at, :], self.weights[UP, 1, block], NT)
+        by = self._quarters(which, 0, 4)
+        into[...] = (dot(by, self.dh[...], TN) if which == DOWN else dot(self.a[...], by, TN)).astype(BF16)
 
     def inputs(self, block, tile):
-        size = self.a.shape[0] // 2
-        at = pl.ds(tile * size, size)
-        self.da[at, :] = jnp.where(block == 0, 0.0, self.da[at, :]) + self._inputs(block, at)
+        part = dot(self._quarters(GATE, 2 * tile, 2), self.weights[GATE, 1, block], NT)
+        part = part + dot(self._quarters(UP, 2 * tile, 2), self.weights[UP, 1, block], NT)
+        at = pl.ds(12 + 2 * tile, 2), pl.ds(0, self.size)
+        self.wide[at] = jnp.where(block == 0, 0.0, self.wide[at]) + part.reshape(2, self.size, BLOCK)
 
     def below(self, tile):
-        size = self.a.shape[0] // 8
+        block, size = self.weights.shape[2] - 1, self.size // 2
 
         def one(i, _):
             at = pl.ds(pl.multiple_of(i * size, size), size)
-            by = (self.da[at, :] + self._inputs(self.weights.shape[2] - 1, at)).astype(BF16).astype(F32)
-            wide = self.states[1, at, :].astype(F32)
+            quarter, rows = lax.div(i, 2), pl.ds(pl.multiple_of(lax.rem(i, 2) * size, size), size)
+            by = self.wide[12 + quarter, rows, :]
+            for which in (GATE, UP):
+                by = by + dot(self.wide[4 * which + quarter, rows, :].astype(BF16), self.weights[which, 1, block], NT)
+            by = by.astype(BF16).astype(F32)
+            wide = self.h[at, :].astype(F32)
             scale = inverse_rms(wide)
             by = by * scale - wide * (scale * scale * scale * jnp.mean(by * wide, -1, keepdims=True))
             self.dh[at, :] = self.dh[at, :] + by.astype(BF16)
-            self.a[at, :] = normed(self.states[0, at, :])
+            self.a[at, :] = normed(self.a[at, :])
             return 0
 
         lax.fori_loop(4 * tile, 4 * tile + 4, one, 0)
+
+
+def moment_blocks(layers, blocks):
+    order = [(number, k, which, j) for number in reversed(range(layers)) for which in range(3) for j in range(blocks) for k in range(2)]
+    places = {}
+    for i, key in enumerate(order):
+        if i < KEPT:
+            places[key] = 0, i
+        elif i < KEPT + 16:
+            places[key] = 1, i - KEPT
+        else:
+            places[key] = 2, i - KEPT - 16
+    return places
 
 
 def block_at(arrays, which, number, j, r0=0, n=BLOCK):
@@ -454,21 +471,21 @@
 
 
 def train_kernel(x, dy, *refs):
-    weights, moments, (g, w, kept), refs = refs[:3], (refs[3:6], refs[6:9]), refs[9:12], refs[12:]
-    (states, dh, a, by, da), scratch = refs[:5], refs[5:]
+    weights, moments, (g, w, kept, wide), refs = refs[:3], (refs[3:6], refs[6:9]), refs[9:13], refs[13:]
+    (dh, h, a), scratch = refs[:3], refs[3:]
     scratch, (send_sems, recv_sems, in_sems) = scratch[:-3], scratch[-3:]
     _, layers, blocks, _, _ = w.shape
     chunks = layers * blocks
     assert layers == 2
     torus = Torus()
     wait_barrier = torus.barrier()
-    size = min(TILE, dh.shape[0])
+    size = dh.shape[0] // 4
 
     def weight(which, number, j):
         return block_at(weights, which, number, j), w.at[which, number, j]
 
-    first = x.at[0, pl.ds(0, size)], states.at[0, pl.ds(0, size)]
-    rest = x.at[0, pl.ds(size, x.shape[1] - size)], states.at[0, pl.ds(size, x.shape[1] - size)]
+    first = x.at[0, pl.ds(0, size)], dh.at[pl.ds(0, size)]
+    rest = x.at[0, pl.ds(size, 3 * size)], dh.at[pl.ds(size, 3 * size)]
     groups = {("x", 0): ([first], first[1])}
     for j in range(blocks):
         groups["in", j] = [weight(which, 0, j) for which in (GATE, UP)], w.at[pl.ds(GATE, 2), 0, j]
@@ -476,12 +493,15 @@
             groups["out", 0] = [weight(DOWN, 0, i) for i in range(blocks)], w.at[DOWN, 0]
     groups["x", 1] = [rest], rest[1]
     groups["late", 0] = [weight(which, 1, j) for j in range(blocks) for which in range(3)], w.at[:, 1]
-    groups["late", 1] = [(dy.at[0], dh)], dh
-    idle = [(block_at(moments[k], i, layers - 1, j), kept.at[k, i, j]) for k in range(2) for i in range(3) for j in range(blocks)]
-    groups["idle", 0] = idle, kept
+    groups["again", 0] = [(x.at[0], a)], a
+    places = moment_blocks(layers, blocks)
+    for n, into in enumerate((kept, wide)):
+        pairs = [(block_at(moments[k], i, number, j), into.at[p]) for (number, k, i, j), (m, p) in places.items() if m == n]
+        groups["moments", n] = pairs, into.at[pl.ds(0, len(pairs))]
     sem_of = {key: i for i, key in enumerate(groups)}
-
-    def begin(key):
+    dy_sem = in_sems.at[len(groups)]
+
+    def begin(*key):
         for src, dst in groups[key][0]:
             pltpu.make_async_copy(src, dst, in_sems.at[sem_of[key]]).start()
 
@@ -490,13 +510,13 @@
         pltpu.make_async_copy(like, like, in_sems.at[sem_of[key]]).wait()
 
     for key in groups:
-        if key[0] != "idle":
-            begin(key)
-    compute = Compute(w, states, dh, a, by, da)
-    compute.forward(wait)
+        if key[0] not in ("again", "moments"):
+            begin(*key)
+    compute = Compute(w, dh, h, a, wide)
+    compute.forward(wait, lambda at: pltpu.make_async_copy(dy.at[0, at, :], dh.at[at, :], dy_sem).start())
     wait("late", 0)
-    wait("late", 1)
-    begin(("idle", 0))
+    pltpu.make_async_copy(dh, dh, dy_sem).wait()
+    begin("moments", 0)
     wait_barrier()
 
     sites, exchanges = [0], []
@@ -523,9 +543,15 @@
 
             @pl.when(c == blocks - 1)
             def _():
+                if tile == "0":
+                    wait("again", 0)
                 compute.below(int(tile))
 
             return
+        if what == LAST:
+            @pl.when(c == blocks - 1)
+            def _():
+                begin("again", 0)
 
         @pl.when(c < chunks)
         def _():
@@ -534,6 +560,11 @@
             else:
                 which = ("down", "gate", "up").index(what)
                 compute.gradient(which, g.at[c, which])
+
+        if what == LAST:
+            @pl.when(c == chunks - 1)
+            def _():
+                begin("moments", 1)
 
     lags = [item[2] for item in PERIOD if not isinstance(item, str)]
 
@@ -558,7 +589,8 @@
         return 0
 
     lax.fori_loop(0, chunks + max(lags), body, 0)
-    wait("idle", 0)
+    wait("moments", 0)
+    wait("moments", 1)
 
 
 def gradients(x, dy, weights, moments):
@@ -566,22 +598,17 @@
     layers, d, ff = gate.shape
     tokens = x.shape[1]
     chunks = layers * ff // BLOCK
-    scratch = [
-        pltpu.VMEM((layers, tokens, d), BF16),
-        pltpu.VMEM((tokens, d), BF16),
-        pltpu.VMEM((tokens, d), BF16),
-        pltpu.VMEM((3, tokens, BLOCK), BF16),
-        pltpu.VMEM((tokens, d), F32),
-    ]
+    scratch = [pltpu.VMEM((tokens, d), BF16) for _ in range(3)]
     n_sites = 0
     for order, chained, _ in COLOURS:
         scratch += Exchange.scratch(order, chained, SLOTS)
         n_sites += Exchange.n_sites(order, chained)
-    scratch += [pltpu.SemaphoreType.DMA((len(COLOURS), chunks)), pltpu.SemaphoreType.DMA((SLOTS, n_sites)), pltpu.SemaphoreType.DMA((11,))]
+    scratch += [pltpu.SemaphoreType.DMA((len(COLOURS), chunks)), pltpu.SemaphoreType.DMA((SLOTS, n_sites)), pltpu.SemaphoreType.DMA((12,))]
     out = [
         pltpu.VMEM((chunks, 3, BLOCK, BLOCK), BF16),
         pltpu.VMEM((3, layers, ff // BLOCK, BLOCK, BLOCK), BF16),
-        pltpu.VMEM((2, 3, ff // BLOCK, BLOCK, BLOCK), F32),
+        pltpu.VMEM((KEPT, BLOCK, BLOCK), F32),
+        pltpu.VMEM((16, BLOCK, BLOCK), F32),
     ]
     return pl.pallas_call(
         train_kernel,
@@ -601,82 +628,80 @@
     return (w - 0.02 * step).astype(BF16), m, v
 
 
-def adamw_kernel(g, w, kept, *refs):
+def adamw_kernel(g, w, kept, wide, *refs):
     moments, new, refs = (refs[:3], refs[3:6]), (refs[6:9], refs[9:12], refs[12:15]), refs[15:]
-    first, *staged, in_sems, out_sems = refs
+    own, *staged, in_sems, out_sems = refs
     _, layers, blocks, _, _ = w.shape
     parts = BLOCK // PIECE
-
-    def load(which, j):
+    places = moment_blocks(layers, blocks)
+
+    def load(key):
+        number, k, which, j = key
+        p = places[key][1]
+        return pltpu.make_async_copy(block_at(moments[k], which, number, j), own.at[p], in_sems.at[p])
+
+    def save(slot, which, number, j, r0):
         return [
-            pltpu.make_async_copy(block_at(moments[k], which, 0, j), first.at[k, which, j], in_sems.at[k, which, j])
-            for k in range(2)
-        ]
-
-    def save(number, slot, which, j, r0):
-        return [
-            pltpu.make_async_copy(staged[k].at[number, slot], block_at(new[k], which, number, j, r0, PIECE), out_sems.at[number, slot, k])
+            pltpu.make_async_copy(staged[k].at[slot], block_at(new[k], which, number, j, r0, PIECE), out_sems.at[slot, k])
             for k in range(3)
         ]
 
-    for which in range(3):
-        for j in range(blocks):
-            for copy in load(which, j):
+    for key, (where, _) in places.items():
+        if where == 2:
+            load(key).start()
+
+    done = 0
+    for number, _, which, j in [key for key in places if key[1] == 0]:
+        here = [places[number, k, which, j] for k in range(2)]
+        for k in range(2):
+            if here[k][0] == 2:
+                load((number, k, which, j)).wait()
+
+        def one(r, _, done=done, number=number, which=which, j=j, here=here):
+            n = done + r
+            slot = lax.rem(n, OUTPUTS)
+
+            @pl.when(n >= OUTPUTS)
+            def _():
+                for copy in save(slot, which, number, j, r * PIECE):
+                    copy.wait()
+
+            for r0 in range(0, PIECE, STRIP):
+                rows = ds(r * PIECE + r0, STRIP)
+                grad = g[(layers - 1 - number) * blocks + j, which, rows, :].astype(F32)
+                m, v = ((kept, wide, own)[where][p, rows, :] for where, p in here)
+                now = adamw(w[which, number, j, rows, :].astype(F32), m, v, grad)
+                for k in range(3):
+                    staged[k][slot, pl.ds(r0, STRIP), :] = now[k]
+            for copy in save(slot, which, number, j, r * PIECE):
                 copy.start()
-
-    for which in range(3):
-
-        def one(i, _, which=which):
-            j, r = lax.div(i, parts), lax.rem(i, parts)
-            slot = lax.rem(i, OUTPUTS)
-
-            @pl.when(r == 0)
-            def _():
-                for copy in load(which, j):
-                    copy.wait()
-
-            for number in reversed(range(layers)):
-
-                @pl.when(which * blocks * parts + i >= OUTPUTS)
-                def _(number=number):
-                    for copy in save(number, slot, which, j, r * PIECE):
-                        copy.wait()
-
-                moment = kept if number else first
-                for r0 in range(0, PIECE, STRIP):
-                    rows = ds(r * PIECE + r0, STRIP)
-                    grad = g[(layers - 1 - number) * blocks + j, which, rows, :].astype(F32)
-                    now = adamw(w[which, number, j, rows, :].astype(F32), moment[0, which, j, rows, :], moment[1, which, j, rows, :], grad)
-                    for k in range(3):
-                        staged[k][number, slot, pl.ds(r0, STRIP), :] = now[k]
-                for copy in save(number, slot, which, j, r * PIECE):
-                    copy.start()
             return 0
 
-        lax.fori_loop(0, blocks * parts, one, 0)
+        lax.fori_loop(0, parts, one, 0)
+        done += parts
     for slot in range(OUTPUTS):
-        for number in range(layers):
-            for copy in save(number, slot, DOWN, 0, 0):
-                copy.wait()
-
-
-def update(g, w, kept, weights, moments):
+        for copy in save(slot, DOWN, 0, 0, 0):
+            copy.wait()
+
+
+def update(g, w, kept, wide, weights, moments):
     _, layers, blocks, _, _ = w.shape
     vmem, hbm = pl.BlockSpec(memory_space=pltpu.VMEM), pl.BlockSpec(memory_space=pltpu.HBM)
+    own = max(1, sum(where == 2 for where, _ in moment_blocks(layers, blocks).values()))
     return pl.pallas_call(
         adamw_kernel,
         out_shape=[jax.ShapeDtypeStruct(a.shape, BF16) for a in weights] + [jax.ShapeDtypeStruct(a.shape, F32) for a in moments],
-        in_specs=[vmem] * 3 + [hbm] * 6,
+        in_specs=[vmem] * 4 + [hbm] * 6,
         out_specs=[hbm] * 9,
         scratch_shapes=[
-            pltpu.VMEM((2, 3, blocks, BLOCK, BLOCK), F32),
-            *(pltpu.VMEM((layers, OUTPUTS, PIECE, BLOCK), dtype) for dtype in (BF16, F32, F32)),
-            pltpu.SemaphoreType.DMA((2, 3, blocks)),
-            pltpu.SemaphoreType.DMA((layers, OUTPUTS, 3)),
+            pltpu.VMEM((own, BLOCK, BLOCK), F32),
+            *(pltpu.VMEM((OUTPUTS, PIECE, BLOCK), dtype) for dtype in (BF16, F32, F32)),
+            pltpu.SemaphoreType.DMA((own,)),
+            pltpu.SemaphoreType.DMA((OUTPUTS, 3)),
         ],
         compiler_params=pltpu.CompilerParams(vmem_limit_bytes=UPDATE_LIMIT),
         name="update",
-    )(g, w, kept, *moments)
+    )(g, w, kept, wide, *moments)
 
 
 def solution(mesh):

time: 167 us -> 164 us (0.982)
  Pallas kernels: 165 us -> 162 us
    pallas_call x1, Pallas kernels: 21 us -> 16.8 us  [update(): pl.pallas_call(adamw_kernel, out_shape=[jax.ShapeDtypeStruct(a.shape, BF1...]
where the time goes in v4:
time: 164 us; the launch traced here: 163 us
  Pallas kernels  162 us (99%)
    pallas_call x1, Pallas kernels, gradients(): pl.pallas_call(train_kernel, out_shape=out, in_specs=[pl.BlockSpec(memory...  145 us
    pallas_call x1, Pallas kernels, update(): pl.pallas_call(adamw_kernel, out_shape=[jax.ShapeDtypeStruct(a.shape, BF1...  16.8 us

profile of v4, /device:TPU:2, one launch (start us, length us, event | category | flops | bytes accessed | tf_op | source)
XLA Modules:
  0.0 162.5 jit_solution(4146093185908108136)
XLA Ops:
  0.6 145.0 %gradients.1 = (bf16[6,3,512,512]{3,2,1,0:T(8,128)(2,1)S(1)}, bf16[3,2,3,512,512]{4,3,2,1,0:T(8,128)(2,1)S(1)}, f32[14,512,512]{2,1,0:T(8,128)S(1)}, f32[16,512,512]{2,1,0:T(8,128)S(1)}) custom-call(bf16[1,2048,512]{2,1,0:T(8,128)(2,1)} %x.1, bf16[1,2048,512]{2,1,0:T(8,128)(2,1)} %dy.1, bf16[2,512,1536]{2,1,0:T(8,128)(2,1)} %refs_0_.2, ...), custom_call_target="tpu_custom_call" | custom-call | tf_op jit(solution)/shard_map/gradients/pallas_call | solution.py:613
  145.6 16.8 %update.1 = (bf16[2,512,1536]{2,1,0:T(8,128)(2,1)}, bf16[2,512,1536]{2,1,0:T(8,128)(2,1)}, bf16[2,1536,512]{2,1,0:T(8,128)(2,1)}, f32[2,512,1536]{2,1,0:T(8,128)...) custom-call(bf16[6,3,512,512]{3,2,1,0:T(8,128)(2,1)S(1)} %get-tuple-, ...), custom_call_target="tpu_custom_call" | custom-call | tf_op jit(solution)/shard_map/update/pallas_call | solution.py:691

commit v5 on v4

--- a/solution.py
+++ b/solution.py
@@ -10,6 +10,7 @@
 MESH = pl.DeviceIdType.MESH
 DIMS = (4, 4, 8)
 BLOCK = 512
+HEAD_START_NS = 2098
 LAST = "down"
 KEPT = 14
 PIECE = 128
@@ -18,23 +19,23 @@
 OUTPUTS = 8
 PERIOD = (
     "back 0",
-    (0, 4, 2), (1, 7, 4), (0, 1, 1), (0, 9, 5),
+    (2, 7, 3), (0, 9, 5),
     "back 1",
-    (2, 2, 1), (2, 5, 2), (1, 9, 5), (0, 6, 3),
+    (1, 4, 2), (1, 1, 1), (2, 2, 1),
     "back 2",
-    (1, 4, 2), (2, 11, 5),
+    (0, 4, 2), (1, 6, 3), (2, 5, 2), (0, 1, 1), (0, 8, 4), (2, 11, 5),
     "back 3",
-    (1, 2, 1), (0, 8, 4), (2, 8, 3),
+    (0, 6, 3), (2, 8, 3), (1, 8, 4),
     "up",
-    (0, 2, 1), (2, 0, 0), (1, 6, 3), (2, 3, 1), (2, 6, 2),
+    (2, 0, 0), (2, 3, 1), (1, 2, 1),
     "gate",
-    (1, 0, 0), (0, 5, 2),
+    (2, 6, 2), (0, 2, 1),
     "down",
-    (1, 8, 4), (1, 5, 2), (2, 10, 4), (0, 0, 0),
+    (1, 5, 2), (0, 10, 5), (1, 0, 0), (0, 5, 2),
     "inputs 0",
-    (0, 3, 1), (2, 12, 5), (2, 1, 0), (1, 10, 5), (2, 4, 1), (2, 7, 2),
+    (2, 10, 4), (0, 7, 3), (1, 3, 1), (2, 1, 0), (1, 10, 5), (0, 0, 0), (2, 4, 1), (1, 7, 3), (2, 12, 5), (2, 9, 3),
     "inputs 1",
-    (2, 9, 3), (1, 3, 1), (0, 7, 3), (0, 10, 5), (1, 1, 0),
+    (0, 3, 1), (1, 9, 4),
 )
 VMEM_LIMIT = UPDATE_LIMIT = 16_700_000
 TN = (((0,), (0,)), ((), ()))
@@ -513,6 +514,11 @@
         if key[0] not in ("again", "moments"):
             begin(*key)
     compute = Compute(w, dh, h, a, wide)
+
+    @pl.when(lax.axis_index("rep") == 1)
+    def _():
+        pl.delay(HEAD_START_NS)
+
     compute.forward(wait, lambda at: pltpu.make_async_copy(dy.at[0, at, :], dh.at[at, :], dy_sem).start())
     wait("late", 0)
     pltpu.make_async_copy(dh, dh, dy_sem).wait()

time: 164 us -> 166 us (1.012)
  Pallas kernels: 162 us -> 165 us
    pallas_call x1, Pallas kernels: 145 us -> 148 us  [gradients(): pl.pallas_call(train_kernel, out_shape=out, in_specs=[pl.BlockSpec(memory...]
where the time goes in v5:
time: 166 us
  Pallas kernels  165 us (99%)
    pallas_call x1, Pallas kernels, gradients(): pl.pallas_call(train_kernel, out_shape=out, in_specs=[pl.BlockSpec(memory...  148 us
    pallas_call x1, Pallas kernels, update(): pl.pallas_call(adamw_kernel, out_shape=[jax.ShapeDtypeStruct(a.shape, BF1...  16.8 us

profile of v5, /device:TPU:2, one launch (start us, length us, event | category | flops | bytes accessed | tf_op | source)
XLA Modules:
  0.0 165.5 jit_solution(12231182402434986245)
XLA Ops:
  0.6 147.9 %gradients.1 = (bf16[6,3,512,512]{3,2,1,0:T(8,128)(2,1)S(1)}, bf16[3,2,3,512,512]{4,3,2,1,0:T(8,128)(2,1)S(1)}, f32[14,512,512]{2,1,0:T(8,128)S(1)}, f32[16,512,512]{2,1,0:T(8,128)S(1)}) custom-call(bf16[1,2048,512]{2,1,0:T(8,128)(2,1)} %x.1, bf16[1,2048,512]{2,1,0:T(8,128)(2,1)} %dy.1, bf16[2,512,1536]{2,1,0:T(8,128)(2,1)} %refs_0_.2, ...), custom_call_target="tpu_custom_call" | custom-call | tf_op jit(solution)/shard_map/gradients/pallas_call | solution.py:619
  148.6 16.8 %update.1 = (bf16[2,512,1536]{2,1,0:T(8,128)(2,1)}, bf16[2,512,1536]{2,1,0:T(8,128)(2,1)}, bf16[2,1536,512]{2,1,0:T(8,128)(2,1)}, f32[2,512,1536]{2,1,0:T(8,128)...) custom-call(bf16[6,3,512,512]{3,2,1,0:T(8,128)(2,1)S(1)} %get-tuple-, ...), custom_call_target="tpu_custom_call" | custom-call | tf_op jit(solution)/shard_map/update/pallas_call | solution.py:697
